TPU v7x, 512 devices: a whole 4x8x8 slice. The times are simulated.
512 devices in a mesh: dom: 64 (over x, y, core), grp: 8 (over z).
Axes of the slice: x: 4, y: 8, z: 8, core: 2. Of those that a mesh axis runs over, the one named last changes fastest.
Arguments:
- tangent_tiles: bfloat16 [65536, 128, 128], P(('grp', 'dom')), parts along dimension 0, may hold values from -0.5 to 0.5
- tile_blocks: int32 [8192, 2], P('dom'), may hold values from 0 to 511, as said below
- block_home: int32 [512], replicated, may hold values from 0 to 511, as said below
- tile_count: int32 [64], P('dom'), may hold values from 48 to 128, as said below
- basis: bfloat16 [65536, 256], P('dom'), may hold values from -0.29882812 to 0.29882812
Outputs:
- reduced: float32 [2048, 256], P('grp'), parts along dimension 0
There are 8 independent parts, one for each index of `grp`. A program takes and returns all parts, laid end to end along the dimension named above; an argument that names none is the same for every part. Nothing has to cross between parts.
Inputs may be any that keep to these rules, and one draw needn't show every extreme that they name: `tile_blocks`: every row block named by a device's tile slots has its position held by one of the devices with dom index from that device's index - 4 to its index + 8 // 2 - 1, taken cyclically. Among the row blocks named by one device's 128 slots, at most 2 distinct ones have their position held by any one device; every device reaches 2 for some holder. `block_home`: A permutation of the row blocks. `tile_count`: some device has exactly 128 live slots.
All inputs are finite; a program needn't handle non-finite values.
Results may differ from a plain program's by a relative error of at most 0.0029.
Values may be sent and summed in bfloat16 or wider, within the bound.
No kernel may reach another device: no remote copies, remote signals or barrier semaphores. Data moves between devices by JAX's collectives and lax.ppermute only.
A program may use at most 64 MiB of HBM per device.

v0:
```python
import jax
import jax.numpy as jnp
from jax import lax
from jax.experimental import pallas as pl
from jax.experimental.pallas import tpu as pltpu
from jax.sharding import PartitionSpec as P


CAP = 2
NEAR = 8
SLOTS = NEAR * CAP
GROUP = 4
UNROLL = 4


def tables_kernel(me_ref, links_in, home_in, own, slots_ref, ids_ref, asks_ref, copy_ref, links_ref, home_ref, sems):
    loads = [
        pltpu.make_async_copy(links_in, links_ref, sems.at[0]),
        pltpu.make_async_copy(home_in, home_ref, sems.at[1]),
    ]
    for load in loads:
        load.start()
    store = pltpu.make_async_copy(own, copy_ref, sems.at[2])
    store.start()
    for load in loads:
        load.wait()
    me = me_ref[0]
    core = me % 2
    links = links_ref[...]
    tiles = links.shape[1]
    n_home, lanes = home_ref.shape
    n_rel = NEAR * 8
    high = links // lanes
    low = links % lanes
    place = jnp.zeros_like(links)
    for part in range(n_home):
        row = jnp.broadcast_to(home_ref[part : part + 1, :], links.shape)
        found = jnp.take_along_axis(row, low, axis=1)
        place = jnp.where(high == part, found, place)
    ndom = n_home * lanes // 8
    window = (place // 8 - me + NEAR // 2 + ndom) % ndom
    window = jnp.where((window % 2 == 1) & (core == 1), (window + 2) % NEAR, window)
    rel = window * 8 + place % 8
    index = lax.broadcasted_iota(jnp.int32, (n_rel, tiles), 0)
    lane = lax.broadcasted_iota(jnp.int32, (n_rel, tiles), 1)
    hit_row = index == rel[0:1, :]
    hit_col = index == rel[1:2, :]
    hits = jnp.where(hit_row | hit_col, 1.0, 0.0)
    wanted = jnp.broadcast_to(jnp.max(hits, axis=1, keepdims=True), (n_rel, tiles))
    a = lax.broadcasted_iota(jnp.int32, (n_rel, n_rel), 0)
    b = lax.broadcasted_iota(jnp.int32, (n_rel, n_rel), 1)
    before = jnp.where((a // 8 == b // 8) & (b < a), 1.0, 0.0)
    level = jnp.dot(before, wanted, preferred_element_type=jnp.float32)
    slot = (index // 8) * CAP + level.astype(jnp.int32)
    row_slot = jnp.sum(jnp.where(hit_row, slot, 0), axis=0, keepdims=True)
    col_slot = jnp.sum(jnp.where(hit_col, slot, 0), axis=0, keepdims=True)
    slots_ref[0:1, :] = row_slot
    slots_ref[1:2, :] = col_slot
    ids = jnp.sum(jnp.where((wanted > 0.5) & (slot == lane), index % 8, 0), axis=0, keepdims=True)
    ids_ref[...] = ids
    asks_ref[...] = jnp.broadcast_to(ids[None], asks_ref.shape)
    store.wait()


def order_kernel(count_ref, slots_ref, order_ref):
    tiles = slots_ref.shape[1]
    spots = order_ref.shape[1]
    rows = 2 * SLOTS
    live = lax.broadcasted_iota(jnp.int32, (1, tiles), 1) < count_ref[0]
    row = jnp.where(live, slots_ref[0:1, :], SLOTS)
    hit = lax.broadcasted_iota(jnp.int32, (rows, tiles), 0) == row
    ones = jnp.where(hit, 1.0, 0.0)
    counts = jnp.sum(ones, axis=1, keepdims=True).astype(jnp.int32)
    groups = jnp.broadcast_to((counts + GROUP - 1) // GROUP, (rows, tiles))
    groups = jnp.where(lax.broadcasted_iota(jnp.int32, (rows, tiles), 0) < SLOTS, groups, 0).astype(jnp.float32)
    a = lax.broadcasted_iota(jnp.int32, (rows, rows), 0)
    b = lax.broadcasted_iota(jnp.int32, (rows, rows), 1)
    first = jnp.dot(jnp.where(b < a, 1.0, 0.0), groups, preferred_element_type=jnp.float32)
    a = lax.broadcasted_iota(jnp.int32, (tiles, tiles), 0)
    b = lax.broadcasted_iota(jnp.int32, (tiles, tiles), 1)
    rank = jnp.dot(ones, jnp.where(a < b, 1.0, 0.0), preferred_element_type=jnp.float32)
    spot = jnp.sum(jnp.where(hit, first * GROUP + rank, 0.0), axis=0, keepdims=True).astype(jnp.int32)
    spot = jnp.where(row < SLOTS, spot, -1)
    at = jnp.where(lax.broadcasted_iota(jnp.int32, (spots, tiles), 0) == spot, 1.0, 0.0)
    kind = lax.broadcasted_iota(jnp.int32, (8, tiles), 0)
    tile = lax.broadcasted_iota(jnp.int32, (8, tiles), 1)
    col = jnp.broadcast_to(slots_ref[1:2, :], (8, tiles)) - SLOTS
    values = jnp.where(kind == 0, tile, jnp.where(kind == 1, col, jnp.broadcast_to(row, (8, tiles))))
    found = lax.dot_general(
        values.astype(jnp.float32), at, (((1,), (1,)), ((), ())), preferred_element_type=jnp.float32
    ).astype(jnp.int32)
    kind = lax.broadcasted_iota(jnp.int32, (8, spots), 0)
    n_groups = jnp.sum(groups[:, 0:1], axis=0, keepdims=True).astype(jnp.int32)
    found = jnp.where(kind == 1, found + SLOTS, found)
    order_ref[...] = jnp.where(kind == 3, n_groups, found)


def serve_kernel(me_ref, asks_ref, own, other, out_a, out_b, out_c, asked, sems):
    ndom = asks_ref.shape[0]
    me = me_ref[0]
    core = me % 2
    ahead = jnp.where(core == 0, 1, ndom - 1)
    near = me + 2 * ahead
    who = (near % ndom, (near + 1 - 2 * core) % ndom, (me + 4 * ahead) % ndom, (me + 4) % ndom)
    fetch = [pltpu.make_async_copy(asks_ref.at[w], asked.at[i], sems.at[i]) for i, w in enumerate(who)]
    for copy in fetch:
        copy.start()
    for copy in fetch:
        copy.wait()
    base = jnp.where(core == 0, 2, 6) * CAP
    for j in range(CAP):
        out_a[j] = own[asked[0, 0, base + j]]
        out_a[CAP + j] = other[asked[0, 0, base + CAP + j]]
        out_a[2 * CAP + j] = other[asked[1, 0, base + j]]
        out_a[3 * CAP + j] = own[asked[1, 0, base + CAP + j]]
        out_b[j] = own[asked[2, 0, j]]
        out_b[CAP + j] = other[asked[2, 0, CAP + j]]
        out_c[j] = own[asked[3, 0, j]]


def project_kernel(me_ref, order_in, ids_in, tiles, own, other, in_a, in_s, in_b, in_c, out_ref,
                   order, ids, blocks, sums, sems):
    block = tiles.shape[1]
    tabs = [pltpu.make_async_copy(order_in, order, sems.at[0]), pltpu.make_async_copy(ids_in, ids, sems.at[1])]
    for copy in tabs:
        copy.start()
    core = me_ref[0] % 2
    blocks[pl.ds((2 + 4 * core) * CAP, 2 * CAP)] = in_a[pl.ds(0, 2 * CAP)]
    blocks[pl.ds((6 - 4 * core) * CAP, 2 * CAP)] = in_s[...]
    blocks[pl.ds(CAP, CAP)] = in_b[pl.ds(CAP, CAP)]

    @pl.when(core == 0)
    def _():
        blocks[pl.ds(0, CAP)] = in_b[pl.ds(0, CAP)]

    @pl.when(core == 1)
    def _():
        blocks[pl.ds(0, CAP)] = in_c[...]

    blocks[SLOTS] = jnp.zeros_like(blocks[SLOTS])
    sums[...] = jnp.zeros_like(sums)
    for copy in tabs:
        copy.wait()
    for j in range(CAP):
        blocks[4 * CAP + j] = own[ids[0, 4 * CAP + j]]
        blocks[5 * CAP + j] = other[ids[0, 5 * CAP + j]]

    def step(s, carry):
        for k in range(UNROLL):
            begin = (s * UNROLL + k) * GROUP
            left = [tiles[order[0, begin + u]] for u in range(GROUP)]
            right = [blocks[order[1, begin + u]] for u in range(GROUP)]
            row = order[2, begin]
            sums[row] = sums[row] + jnp.dot(
                jnp.concatenate(left, axis=1), jnp.concatenate(right, axis=0), preferred_element_type=jnp.float32
            )
        return carry

    lax.fori_loop(0, (order[3, 0] + UNROLL - 1) // UNROLL, step, 0)
    rank = out_ref.shape[1]
    left = blocks[pl.ds(0, SLOTS)].reshape(SLOTS * block, rank)
    total = sums[...].reshape(SLOTS * block, rank)
    high = total.astype(jnp.bfloat16)
    low = (total - high.astype(jnp.float32)).astype(jnp.bfloat16)
    both = lax.dot_general(
        left, jnp.concatenate([high, low], axis=1), (((0,), (0,)), ((), ())), preferred_element_type=jnp.float32
    )
    out_ref[...] = both[:, :rank] + both[:, rank:]


def in_hbm(x):
    return pltpu.with_memory_space_constraint(x, pltpu.HBM)


def on_device(tangent_tiles, tile_blocks, block_home, tile_count, basis):
    ndom = lax.axis_size("dom")
    n_tiles = tangent_tiles.shape[0]
    block = tangent_tiles.shape[1]
    rank = basis.shape[1]
    blk_dev = basis.shape[0] // block
    bf16 = jnp.bfloat16
    anywhere = pl.BlockSpec(memory_space=pltpu.HBM)
    smem = pl.BlockSpec(memory_space=pltpu.SMEM)
    vmem = pl.BlockSpec(memory_space=pltpu.VMEM)
    own = basis.reshape(blk_dev, block, rank)
    pair = [(i, i ^ 1) for i in range(ndom)]
    other = lax.ppermute(own, "dom", pair)
    stored = in_hbm(own)
    me = lax.axis_index("dom").astype(jnp.int32).reshape(1)
    slots, ids, asks, near = pl.pallas_call(
        tables_kernel,
        out_shape=(
            jax.ShapeDtypeStruct((2, n_tiles), jnp.int32),
            jax.ShapeDtypeStruct((1, n_tiles), jnp.int32),
            jax.ShapeDtypeStruct((ndom, 1, n_tiles), jnp.int32),
            jax.ShapeDtypeStruct(own.shape, bf16),
        ),
        in_specs=[smem, anywhere, anywhere, anywhere],
        out_specs=(vmem, vmem, vmem, vmem),
        scratch_shapes=[
            pltpu.VMEM((2, n_tiles), jnp.int32),
            pltpu.VMEM((ndom * blk_dev // 128, 128), jnp.int32),
            pltpu.SemaphoreType.DMA((3,)),
        ],
        compiler_params=pltpu.CompilerParams(vmem_limit_bytes=4 << 20),
        name="tables",
    )(me, in_hbm(tile_blocks.T), in_hbm(block_home.reshape(-1, 128)), stored)
    asks = lax.all_to_all(asks, "dom", 0, 0, tiled=True)
    order = pl.pallas_call(
        order_kernel,
        out_shape=jax.ShapeDtypeStruct((8, 2 * n_tiles), jnp.int32),
        in_specs=[smem, vmem],
        out_specs=vmem,
        cost_estimate=pl.CostEstimate(flops=10**9, transcendentals=0, bytes_accessed=10**4),
        compiler_params=pltpu.CompilerParams(vmem_limit_bytes=4 << 20),
        name="order",
    )(tile_count, slots)

    def split(steps):
        return [(i, (i + (steps if i % 2 == 0 else -steps)) % ndom) for i in range(ndom)]

    def blocks_of(count):
        return jax.ShapeDtypeStruct((count * CAP, block, rank), bf16)

    out_a, out_b, out_c = pl.pallas_call(
        serve_kernel,
        out_shape=(blocks_of(4), blocks_of(2), blocks_of(1)),
        in_specs=[smem] + [vmem] * 3,
        out_specs=(vmem,) * 3,
        scratch_shapes=[pltpu.SMEM((4, 1, n_tiles), jnp.int32), pltpu.SemaphoreType.DMA((4,))],
        compiler_params=pltpu.CompilerParams(vmem_limit_bytes=8 << 20),
        name="serve",
    )(me, asks, near, other)
    in_a = lax.ppermute(out_a, "dom", split(2))
    in_b = lax.ppermute(out_b, "dom", split(4))
    in_c = lax.ppermute(out_c, "dom", [(i, (i + 4) % ndom) for i in range(1, ndom, 2)])
    in_s = lax.ppermute(in_a[2 * CAP :], "dom", pair)
    partial_sum = pl.pallas_call(
        project_kernel,
        out_shape=jax.ShapeDtypeStruct((rank, rank), jnp.float32),
        in_specs=[smem] + [vmem] * 9,
        out_specs=vmem,
        scratch_shapes=[
            pltpu.SMEM((8, 2 * n_tiles), jnp.int32),
            pltpu.SMEM((1, n_tiles), jnp.int32),
            pltpu.VMEM((SLOTS + 1, block, rank), bf16),
            pltpu.VMEM((SLOTS, block, rank), jnp.float32),
            pltpu.SemaphoreType.DMA((2,)),
        ],
        compiler_params=pltpu.CompilerParams(vmem_limit_bytes=24 << 20),
        name="project",
    )(me, order, ids, tangent_tiles, near, other, in_a, in_s, in_b, in_c)
    cut = partial_sum.reshape(rank // 8, 8, rank // 128, 128).transpose(0, 2, 1, 3).reshape(ndom, 8, 128)
    parts = lax.all_to_all(cut, "dom", 0, 0, tiled=True)
    mine = jnp.sum(parts, axis=0)
    copies = jnp.broadcast_to(mine, (ndom, 8, 128))
    whole = lax.all_to_all(copies, "dom", 0, 0, tiled=True)
    return whole.reshape(rank // 8, rank // 128, 8, 128).transpose(0, 2, 1, 3).reshape(rank, rank)


def solution(mesh):
    return jax.shard_map(
        on_device,
        mesh=mesh,
        in_specs=(P(("grp", "dom"), None, None), P("dom", None), P(), P("dom"), P("dom", None)),
        out_specs=P("grp", None),
        check_vma=False,
    )
```

profile of v0, /device:TPU:1, one launch (start us, length us, event | category | flops | bytes accessed | tf_op | source)
XLA Modules:
  0.0 90.8 jit_solution(16386580720899990680)
XLA Ops:
  0.0 8.7 %collective-permute-start = (bf16[8,128,256]{2,1,0:T(8,128)(2,1)}, bf16[8,128,256]{2,1,0:T(8,128)(2,1)S(1)}, u32[]{:S(2)}, u32[]{:S(2)}) collective-permute-start(bf16[8,128,256]{2,1,0:T(8,128)(2,1)} %bitcast.16), channel_id=1, source_target_pairs={{0,8},{8,0},{16,24},{24,16},{32,40},{40,32},{48,56},{56,48},{64,72... | collective-permute-start | bytes 1572872 | tf_op jit(solution)/shard_map/ppermute | solution.py:187
  8.7 0.0 copy-start
  8.8 1.3 %tables.1 = (s32[2,128]{1,0:T(2,128)S(1)}, s32[1,128]{1,0:T(1,128)S(1)}, s32[64,1,128]{2,1,0:T(1,128)S(1)}, bf16[8,128,256]{2,1,0:T(8,128)(2,1)S(1)}) custom-call(s32[1]{0:T(128)} %bitcast.me_ref, s32[2,128]{1,0:T(2,128)} %bitcast.19, s32[4,128]{1,0:T(4,128)} %bitcast.18, bf16[8,128,256]{2,1,0:T(8,128)(2,1)} %bitcast.17), custom_call_target="tpu_custom_call" | custom-call | tf_op jit(solution)/shard_map/tables/pallas_call | solution.py:190
  10.0 14.1 %all_to_all.15.asks_ref = s32[64,1,128]{2,1,0:T(1,128)S(1)} all-to-all(s32[64,1,128]{2,1,0:T(1,128)S(1)} %get-tuple-element.15), channel_id=1, replica_groups=mesh['dom'=64,'grp'=8] {'dom'}, dimensions={0} | all-to-all | bytes 65536 | tf_op jit(solution)/shard_map/all_to_all | solution.py:208
  24.2 0.0 collective-permute-done.other
  24.2 0.7 serve.1
  24.8 2.8 %collective-permute-start.1 = (bf16[8,128,256]{2,1,0:T(8,128)(2,1)S(1)}, bf16[8,128,256]{2,1,0:T(8,128)(2,1)S(1)}, u32[]{:S(2)}, u32[]{:S(2)}) collective-permute-start(bf16[8,128,256]{2,1,0:T(8,128)(2,1)S(1)} %get-tuple-element.16), channel_id=1, source_target_pairs={{0,16},{8,504},{16,32},{24,8},{32,48},{40,24},{48,64},{56,40},{64,... | collective-permute-start | bytes 1572872 | tf_op jit(solution)/shard_map/ppermute | solution.py:234
  27.6 2.2 %collective-permute-start.3 = (bf16[4,128,256]{2,1,0:T(8,128)(2,1)S(1)}, bf16[4,128,256]{2,1,0:T(8,128)(2,1)S(1)}, u32[]{:S(2)}, u32[]{:S(2)}) collective-permute-start(bf16[4,128,256]{2,1,0:T(8,128)(2,1)S(1)} %get-tuple-element.17), channel_id=1, source_target_pairs={{0,32},{8,488},{16,48},{24,504},{32,64},{40,8},{48,80},{56,24},{64... | collective-permute-start | bytes 786440 | tf_op jit(solution)/shard_map/ppermute | solution.py:235
  29.8 5.3 %collective-permute-done.1.in_a = bf16[8,128,256]{2,1,0:T(8,128)(2,1)S(1)} collective-permute-done((bf16[8,128,256]{2,1,0:T(8,128)(2,1)S(1)}, bf16[8,128,256]{2,1,0:T(8,128)(2,1)S(1)}, u32[]{:S(2)}, u32[]{:S(2)}) %collective-permute-start.1) | collective-permute-done | bytes 524320 | tf_op jit(solution)/shard_map/ppermute | solution.py:234
  35.1 9.0 %collective-permute-start.2 = (bf16[4,128,256]{2,1,0:T(8,128)(2,1)S(1)}, bf16[4,128,256]{2,1,0:T(8,128)(2,1)S(1)}, u32[]{:S(2)}, u32[]{:S(2)}) collective-permute-start(bf16[4,128,256]{2,1,0:T(8,128)(2,1)S(1)} %slice.4), channel_id=1, source_target_pairs={{0,8},{8,0},{16,24},{24,16},{32,40},{40,32},{48,56},{56,48},{64,72... | collective-permute-start | bytes 786440 | tf_op jit(solution)/shard_map/ppermute | solution.py:237
  44.1 1.9 %collective-permute-start.4 = (bf16[2,128,256]{2,1,0:T(8,128)(2,1)S(1)}, bf16[2,128,256]{2,1,0:T(8,128)(2,1)S(1)}, u32[]{:S(2)}, u32[]{:S(2)}) collective-permute-start(bf16[2,128,256]{2,1,0:T(8,128)(2,1)S(1)} %get-tuple-element.18), channel_id=1, source_target_pairs={{8,40},{24,56},{40,72},{56,88},{72,104},{88,120},{104,136},{120,15... | collective-permute-start | bytes 393224 | tf_op jit(solution)/shard_map/ppermute | solution.py:236
  46.7 0.4 order.1.order_in
  47.0 7.0 %collective-permute-done.4.in_c = bf16[2,128,256]{2,1,0:T(8,128)(2,1)S(1)} collective-permute-done((bf16[2,128,256]{2,1,0:T(8,128)(2,1)S(1)}, bf16[2,128,256]{2,1,0:T(8,128)(2,1)S(1)}, u32[]{:S(2)}, u32[]{:S(2)}) %collective-permute-start.4) | collective-permute-done | bytes 131104 | tf_op jit(solution)/shard_map/ppermute | solution.py:236
  54.0 0.0 collective-permute-done.3.in_b
  54.0 0.0 collective-permute-done.2.in_s
  54.0 0.0 copy-done
  54.0 4.0 %project.1 = f32[256,256]{1,0:T(8,128)S(1)} custom-call(s32[1]{0:T(128)} %bitcast.me_ref, s32[8,256]{1,0:T(8,128)S(1)} %order.1.order_in, s32[1,128]{1,0:T(1,128)S(1)} %get-tuple-element.13.ids_in, bf16[128,128,128]{2,1,0:T(8,128)(2,1)S(1)} %copy-done, bf16[8,128,256]{2,1,0:T(8,128)(2,1)S(1)} %get-tuple-element.14.own, ...), custom_call_target="tpu_custom_call" | custom-call | tf_op jit(solution)/shard_map/project/pallas_call | solution.py:238
  58.1 14.1 %all_to_all.16 = f32[64,8,128]{2,1,0:T(8,128)S(1)} all-to-all(f32[64,8,128]{2,1,0:T(8,128)S(1)} %bitcast.14), channel_id=1, replica_groups=mesh['dom'=64,'grp'=8] {'dom'}, dimensions={0} | all-to-all | bytes 524288 | tf_op jit(solution)/shard_map/all_to_all | solution.py:254
  72.1 0.1 reduce_sum.9
  72.2 17.8 %all_to_all.17 = f32[64,8,128]{2,1,0:T(8,128)S(1)} all-to-all(f32[64,8,128]{2,1,0:T(8,128)S(1)} %broadcast_in_dim.3), channel_id=1, replica_groups=mesh['dom'=64,'grp'=8] {'dom'}, dimensions={0} | all-to-all | bytes 524288 | tf_op jit(solution)/shard_map/all_to_all | solution.py:257
  90.1 0.7 copy.8
  (2 shorter events, 0.0 us)
Async XLA Ops:
  0.0 24.2 %collective-permute-start = (bf16[8,128,256]{2,1,0:T(8,128)(2,1)}, bf16[8,128,256]{2,1,0:T(8,128)(2,1)S(1)}, u32[]{:S(2)}, u32[]{:S(2)}) collective-permute-start(bf16[8,128,256]{2,1,0:T(8,128)(2,1)} %bitcast.16), channel_id=1, source_target_pairs={{0,8},{8,0},{16,24},{24,16},{32,40},{40,32},{48,56},{56,48},{64,72... | collective-permute-start | bytes 1572872 | tf_op jit(solution)/shard_map/ppermute | solution.py:187
  8.7 45.3 %copy-start = (bf16[128,128,128]{2,1,0:T(8,128)(2,1)S(1)}, bf16[128,128,128]{2,1,0:T(8,128)(2,1)}, u32[]{:S(2)}) copy-start(bf16[128,128,128]{2,1,0:T(8,128)(2,1)} %tiles.1) | copy-start | bytes 12582916
  24.8 10.2 %collective-permute-start.1 = (bf16[8,128,256]{2,1,0:T(8,128)(2,1)S(1)}, bf16[8,128,256]{2,1,0:T(8,128)(2,1)S(1)}, u32[]{:S(2)}, u32[]{:S(2)}) collective-permute-start(bf16[8,128,256]{2,1,0:T(8,128)(2,1)S(1)} %get-tuple-element.16), channel_id=1, source_target_pairs={{0,16},{8,504},{16,32},{24,8},{32,48},{40,24},{48,64},{56,40},{64,... | collective-permute-start | bytes 1572872 | tf_op jit(solution)/shard_map/ppermute | solution.py:234
  27.6 26.4 %collective-permute-start.3 = (bf16[4,128,256]{2,1,0:T(8,128)(2,1)S(1)}, bf16[4,128,256]{2,1,0:T(8,128)(2,1)S(1)}, u32[]{:S(2)}, u32[]{:S(2)}) collective-permute-start(bf16[4,128,256]{2,1,0:T(8,128)(2,1)S(1)} %get-tuple-element.17), channel_id=1, source_target_pairs={{0,32},{8,488},{16,48},{24,504},{32,64},{40,8},{48,80},{56,24},{64... | collective-permute-start | bytes 786440 | tf_op jit(solution)/shard_map/ppermute | solution.py:235
  35.1 19.0 %collective-permute-start.2 = (bf16[4,128,256]{2,1,0:T(8,128)(2,1)S(1)}, bf16[4,128,256]{2,1,0:T(8,128)(2,1)S(1)}, u32[]{:S(2)}, u32[]{:S(2)}) collective-permute-start(bf16[4,128,256]{2,1,0:T(8,128)(2,1)S(1)} %slice.4), channel_id=1, source_target_pairs={{0,8},{8,0},{16,24},{24,16},{32,40},{40,32},{48,56},{56,48},{64,72... | collective-permute-start | bytes 786440 | tf_op jit(solution)/shard_map/ppermute | solution.py:237
  44.1 9.9 %collective-permute-start.4 = (bf16[2,128,256]{2,1,0:T(8,128)(2,1)S(1)}, bf16[2,128,256]{2,1,0:T(8,128)(2,1)S(1)}, u32[]{:S(2)}, u32[]{:S(2)}) collective-permute-start(bf16[2,128,256]{2,1,0:T(8,128)(2,1)S(1)} %get-tuple-element.18), channel_id=1, source_target_pairs={{8,40},{24,56},{40,72},{56,88},{72,104},{88,120},{104,136},{120,15... | collective-permute-start | bytes 393224 | tf_op jit(solution)/shard_map/ppermute | solution.py:236
where the time goes:
time: 91.1 us; the launch traced here: 90.8 us
  blocking collectives  46 us (50%)
  starting transfers between devices  24.6 us (27%)
  waiting for transfers between devices  12.3 us (14%)
  Pallas kernels  6.32 us (7%)
    all_to_all x1, blocking collectives, on_device(): whole = lax.all_to_all(copies, 'dom', 0, 0, tiled=True)  17.8 us
    all_to_all x1, blocking collectives, on_device(): asks = lax.all_to_all(asks, 'dom', 0, 0, tiled=True)  14.1 us
    all_to_all x1, blocking collectives, on_device(): parts = lax.all_to_all(cut, 'dom', 0, 0, tiled=True)  14.1 us
    ppermute x1, starting transfers between devices, on_device(): in_s = lax.ppermute(in_a[2 * CAP:], 'dom', pair)  9.01 us
    ppermute x1, starting transfers between devices, on_device(): other = lax.ppermute(own, 'dom', pair)  8.73 us
    ppermute x1, waiting for transfers between devices, on_device(): lax.ppermute(out_c, 'dom', [(i, (i + 4) % ndom) for i in range(1, ndom, 2)])  6.98 us
    ppermute x1, waiting for transfers between devices, on_device(): in_a = lax.ppermute(out_a, 'dom', split(2))  5.27 us
    pallas_call x1, Pallas kernels, on_device(): pl.pallas_call(project_kernel, out_shape=jax.ShapeDtypeStruct((rank, rank...  4.03 us
  transfers between devices with their start and end apart: 5, of which 2 were waited for; matrix products, arithmetic and copies ran while one was open for 0% of the time, Pallas kernels for 2%

commit v1 on v0

--- a/solution.py
+++ b/solution.py
@@ -13,7 +13,7 @@
 UNROLL = 4
 
 
-def tables_kernel(me_ref, links_in, home_in, own, slots_ref, ids_ref, asks_ref, copy_ref, links_ref, home_ref, sems):
+def tables_kernel(me_ref, links_in, home_in, own, slots_ref, ids_ref, copy_ref, links_ref, home_ref, sems):
     loads = [
         pltpu.make_async_copy(links_in, links_ref, sems.at[0]),
         pltpu.make_async_copy(home_in, home_ref, sems.at[1]),
@@ -58,7 +58,6 @@
     slots_ref[1:2, :] = col_slot
     ids = jnp.sum(jnp.where((wanted > 0.5) & (slot == lane), index % 8, 0), axis=0, keepdims=True)
     ids_ref[...] = ids
-    asks_ref[...] = jnp.broadcast_to(ids[None], asks_ref.shape)
     store.wait()
 
 
@@ -95,75 +94,69 @@
     order_ref[...] = jnp.where(kind == 3, n_groups, found)
 
 
-def serve_kernel(me_ref, asks_ref, own, other, out_a, out_b, out_c, asked, sems):
-    ndom = asks_ref.shape[0]
-    me = me_ref[0]
-    core = me % 2
-    ahead = jnp.where(core == 0, 1, ndom - 1)
-    near = me + 2 * ahead
-    who = (near % ndom, (near + 1 - 2 * core) % ndom, (me + 4 * ahead) % ndom, (me + 4) % ndom)
-    fetch = [pltpu.make_async_copy(asks_ref.at[w], asked.at[i], sems.at[i]) for i, w in enumerate(who)]
+def serve_kernel(me_ref, ask_x, ask_y, ask_n, left, own, right, out_x, out_y, out_n, asked, sems):
+    core = me_ref[0] % 2
+    fetch = [pltpu.make_async_copy(ask, asked.at[i], sems.at[i]) for i, ask in enumerate((ask_x, ask_y, ask_n))]
     for copy in fetch:
         copy.start()
     for copy in fetch:
         copy.wait()
-    base = jnp.where(core == 0, 2, 6) * CAP
     for j in range(CAP):
-        out_a[j] = own[asked[0, 0, base + j]]
-        out_a[CAP + j] = other[asked[0, 0, base + CAP + j]]
-        out_a[2 * CAP + j] = other[asked[1, 0, base + j]]
-        out_a[3 * CAP + j] = own[asked[1, 0, base + CAP + j]]
-        out_b[j] = own[asked[2, 0, j]]
-        out_b[CAP + j] = other[asked[2, 0, CAP + j]]
-        out_c[j] = own[asked[3, 0, j]]
-
-
-def project_kernel(me_ref, order_in, ids_in, tiles, own, other, in_a, in_s, in_b, in_c, out_ref,
+        out_x[j] = left[asked[0, 0, j]]
+
+    @pl.when(core == 0)
+    def _():
+        for j in range(CAP):
+            out_y[j] = right[asked[1, 0, CAP + j]]
+
+    @pl.when(core == 1)
+    def _():
+        for j in range(CAP):
+            out_y[j] = left[asked[1, 0, CAP + j]]
+
+    for n, source in enumerate((left, own, right)):
+        for j in range(CAP):
+            out_n[n * CAP + j] = source[asked[2, 0, (3 + 2 * n) * CAP + j]]
+
+
+def project_kernel(order_in, ids_in, tiles, left, own, right, in_x, in_y, in_n, out_ref,
                    order, ids, blocks, sums, sems):
     block = tiles.shape[1]
     tabs = [pltpu.make_async_copy(order_in, order, sems.at[0]), pltpu.make_async_copy(ids_in, ids, sems.at[1])]
     for copy in tabs:
         copy.start()
-    core = me_ref[0] % 2
-    blocks[pl.ds((2 + 4 * core) * CAP, 2 * CAP)] = in_a[pl.ds(0, 2 * CAP)]
-    blocks[pl.ds((6 - 4 * core) * CAP, 2 * CAP)] = in_s[...]
-    blocks[pl.ds(CAP, CAP)] = in_b[pl.ds(CAP, CAP)]
-
-    @pl.when(core == 0)
-    def _():
-        blocks[pl.ds(0, CAP)] = in_b[pl.ds(0, CAP)]
-
-    @pl.when(core == 1)
-    def _():
-        blocks[pl.ds(0, CAP)] = in_c[...]
-
+    blocks[pl.ds(0, CAP)] = in_x[...]
+    blocks[pl.ds(CAP, CAP)] = in_y[...]
+    for n in range(3):
+        blocks[pl.ds((3 + 2 * n) * CAP, CAP)] = in_n[pl.ds(n * CAP, CAP)]
     blocks[SLOTS] = jnp.zeros_like(blocks[SLOTS])
     sums[...] = jnp.zeros_like(sums)
     for copy in tabs:
         copy.wait()
-    for j in range(CAP):
-        blocks[4 * CAP + j] = own[ids[0, 4 * CAP + j]]
-        blocks[5 * CAP + j] = other[ids[0, 5 * CAP + j]]
+    for n, source in enumerate((left, own, right)):
+        for j in range(CAP):
+            spot = (2 + 2 * n) * CAP + j
+            blocks[spot] = source[ids[0, spot]]
 
     def step(s, carry):
         for k in range(UNROLL):
             begin = (s * UNROLL + k) * GROUP
-            left = [tiles[order[0, begin + u]] for u in range(GROUP)]
-            right = [blocks[order[1, begin + u]] for u in range(GROUP)]
+            many = [tiles[order[0, begin + u]] for u in range(GROUP)]
+            tall = [blocks[order[1, begin + u]] for u in range(GROUP)]
             row = order[2, begin]
             sums[row] = sums[row] + jnp.dot(
-                jnp.concatenate(left, axis=1), jnp.concatenate(right, axis=0), preferred_element_type=jnp.float32
+                jnp.concatenate(many, axis=1), jnp.concatenate(tall, axis=0), preferred_element_type=jnp.float32
             )
         return carry
 
     lax.fori_loop(0, (order[3, 0] + UNROLL - 1) // UNROLL, step, 0)
     rank = out_ref.shape[1]
-    left = blocks[pl.ds(0, SLOTS)].reshape(SLOTS * block, rank)
+    rows = blocks[pl.ds(0, SLOTS)].reshape(SLOTS * block, rank)
     total = sums[...].reshape(SLOTS * block, rank)
     high = total.astype(jnp.bfloat16)
     low = (total - high.astype(jnp.float32)).astype(jnp.bfloat16)
     both = lax.dot_general(
-        left, jnp.concatenate([high, low], axis=1), (((0,), (0,)), ((), ())), preferred_element_type=jnp.float32
+        rows, jnp.concatenate([high, low], axis=1), (((0,), (0,)), ((), ())), preferred_element_type=jnp.float32
     )
     out_ref[...] = both[:, :rank] + both[:, rank:]
 
@@ -183,20 +176,23 @@
     smem = pl.BlockSpec(memory_space=pltpu.SMEM)
     vmem = pl.BlockSpec(memory_space=pltpu.VMEM)
     own = basis.reshape(blk_dev, block, rank)
-    pair = [(i, i ^ 1) for i in range(ndom)]
-    other = lax.ppermute(own, "dom", pair)
+
+    def shift(steps):
+        return [(i, (i + steps) % ndom) for i in range(ndom)]
+
+    left = lax.ppermute(own, "dom", shift(2))
+    right = lax.ppermute(own, "dom", shift(-2))
     stored = in_hbm(own)
     me = lax.axis_index("dom").astype(jnp.int32).reshape(1)
-    slots, ids, asks, near = pl.pallas_call(
+    slots, ids, near = pl.pallas_call(
         tables_kernel,
         out_shape=(
             jax.ShapeDtypeStruct((2, n_tiles), jnp.int32),
             jax.ShapeDtypeStruct((1, n_tiles), jnp.int32),
-            jax.ShapeDtypeStruct((ndom, 1, n_tiles), jnp.int32),
             jax.ShapeDtypeStruct(own.shape, bf16),
         ),
         in_specs=[smem, anywhere, anywhere, anywhere],
-        out_specs=(vmem, vmem, vmem, vmem),
+        out_specs=(vmem, vmem, vmem),
         scratch_shapes=[
             pltpu.VMEM((2, n_tiles), jnp.int32),
             pltpu.VMEM((ndom * blk_dev // 128, 128), jnp.int32),
@@ -205,7 +201,9 @@
         compiler_params=pltpu.CompilerParams(vmem_limit_bytes=4 << 20),
         name="tables",
     )(me, in_hbm(tile_blocks.T), in_hbm(block_home.reshape(-1, 128)), stored)
-    asks = lax.all_to_all(asks, "dom", 0, 0, tiled=True)
+    ask_x = lax.ppermute(ids, "dom", shift(-2))
+    ask_y = lax.ppermute(ids, "dom", [(i, (i + (1 if i % 2 else -1)) % ndom) for i in range(ndom)])
+    ask_n = lax.ppermute(ids, "dom", [(i, i ^ 1) for i in range(ndom)])
     order = pl.pallas_call(
         order_kernel,
         out_shape=jax.ShapeDtypeStruct((8, 2 * n_tiles), jnp.int32),
@@ -216,29 +214,25 @@
         name="order",
     )(tile_count, slots)
 
-    def split(steps):
-        return [(i, (i + (steps if i % 2 == 0 else -steps)) % ndom) for i in range(ndom)]
-
     def blocks_of(count):
         return jax.ShapeDtypeStruct((count * CAP, block, rank), bf16)
 
-    out_a, out_b, out_c = pl.pallas_call(
+    out_x, out_y, out_n = pl.pallas_call(
         serve_kernel,
-        out_shape=(blocks_of(4), blocks_of(2), blocks_of(1)),
-        in_specs=[smem] + [vmem] * 3,
+        out_shape=(blocks_of(1), blocks_of(1), blocks_of(3)),
+        in_specs=[smem] + [vmem] * 6,
         out_specs=(vmem,) * 3,
-        scratch_shapes=[pltpu.SMEM((4, 1, n_tiles), jnp.int32), pltpu.SemaphoreType.DMA((4,))],
+        scratch_shapes=[pltpu.SMEM((3, 1, n_tiles), jnp.int32), pltpu.SemaphoreType.DMA((3,))],
         compiler_params=pltpu.CompilerParams(vmem_limit_bytes=8 << 20),
         name="serve",
-    )(me, asks, near, other)
-    in_a = lax.ppermute(out_a, "dom", split(2))
-    in_b = lax.ppermute(out_b, "dom", split(4))
-    in_c = lax.ppermute(out_c, "dom", [(i, (i + 4) % ndom) for i in range(1, ndom, 2)])
-    in_s = lax.ppermute(in_a[2 * CAP :], "dom", pair)
+    )(me, ask_x, ask_y, ask_n, left, near, right)
+    in_x = lax.ppermute(out_x, "dom", shift(2))
+    in_y = lax.ppermute(out_y, "dom", [(i, (i + (1 if i % 2 else -1)) % ndom) for i in range(ndom)])
+    in_n = lax.ppermute(out_n, "dom", [(i, i ^ 1) for i in range(ndom)])
     partial_sum = pl.pallas_call(
         project_kernel,
         out_shape=jax.ShapeDtypeStruct((rank, rank), jnp.float32),
-        in_specs=[smem] + [vmem] * 9,
+        in_specs=[vmem] * 9,
         out_specs=vmem,
         scratch_shapes=[
             pltpu.SMEM((8, 2 * n_tiles), jnp.int32),
@@ -249,7 +243,7 @@
         ],
         compiler_params=pltpu.CompilerParams(vmem_limit_bytes=24 << 20),
         name="project",
-    )(me, order, ids, tangent_tiles, near, other, in_a, in_s, in_b, in_c)
+    )(order, ids, tangent_tiles, left, near, right, in_x, in_y, in_n)
     cut = partial_sum.reshape(rank // 8, 8, rank // 128, 128).transpose(0, 2, 1, 3).reshape(ndom, 8, 128)
     parts = lax.all_to_all(cut, "dom", 0, 0, tiled=True)
     mine = jnp.sum(parts, axis=0)

time: 91.1 us -> 82.6 us (0.907)
  blocking collectives: 46 us -> 36.8 us
  starting transfers between devices: 24.6 us -> 30.9 us
  waiting for transfers between devices: 12.3 us -> 6.5 us
    all_to_all x1 -> x0, blocking collectives: 14.1 us -> none  [on_device(): asks = lax.all_to_all(asks, 'dom', 0, 0, tiled=True)]
    ppermute x5 -> x8, starting transfers between devices: 24.6 us -> 30.9 us  [the longest x1 8.06 us: on_device(): lax.ppermute(ids, 'dom', [(i, (i + (1 if i % 2 else -1)) % ndom) for i in...]
    ppermute x5 -> x8, waiting for transfers between devices: 12.3 us -> 6.5 us  [the longest x1 5.37 us: on_device(): in_x = lax.ppermute(out_x, 'dom', shift(2))]
    all_to_all x1, blocking collectives: 14.1 us -> 19 us  [on_device(): parts = lax.all_to_all(cut, 'dom', 0, 0, tiled=True)]
  transfers between devices with their start and end apart: 5 -> 8, of which waited for: 2 -> 2; matrix products, arithmetic and copies ran while one was open for 0% -> 0% of each run, Pallas kernels for 2% -> 2%
where the time goes in v1:
time: 82.6 us; the launch traced here: 82.2 us
  blocking collectives  36.8 us (45%)
  starting transfers between devices  30.9 us (37%)
  waiting for transfers between devices  6.5 us (8%)
  Pallas kernels  6.43 us (8%)
    all_to_all x1, blocking collectives, on_device(): parts = lax.all_to_all(cut, 'dom', 0, 0, tiled=True)  19 us
    all_to_all x1, blocking collectives, on_device(): whole = lax.all_to_all(copies, 'dom', 0, 0, tiled=True)  17.8 us
    ppermute x1, starting transfers between devices, on_device(): lax.ppermute(ids, 'dom', [(i, (i + (1 if i % 2 else -1)) % ndom) for i in...  8.06 us
    ppermute x1, starting transfers between devices, on_device(): right = lax.ppermute(own, 'dom', shift(-2))  6.01 us
    ppermute x1, waiting for transfers between devices, on_device(): in_x = lax.ppermute(out_x, 'dom', shift(2))  5.37 us
    pallas_call x1, Pallas kernels, on_device(): pl.pallas_call(project_kernel, out_shape=jax.ShapeDtypeStruct((rank, rank...  4.16 us
    ppermute x1, starting transfers between devices, on_device(): left = lax.ppermute(own, 'dom', shift(2))  4.01 us
    ppermute x1, starting transfers between devices, on_device(): in_n = lax.ppermute(out_n, 'dom', [(i, i ^ 1) for i in range(ndom)])  3.54 us
  transfers between devices with their start and end apart: 8, of which 2 were waited for; matrix products, arithmetic and copies ran while one was open for 0% of the time, Pallas kernels for 2%

profile of v1, /device:TPU:1, one launch (start us, length us, event | category | flops | bytes accessed | tf_op | source)
XLA Modules:
  0.0 82.2 jit_solution(9576632873277444857)
XLA Ops:
  0.0 4.0 %collective-permute-start = (bf16[8,128,256]{2,1,0:T(8,128)(2,1)}, bf16[8,128,256]{2,1,0:T(8,128)(2,1)S(1)}, u32[]{:S(2)}, u32[]{:S(2)}) collective-permute-start(bf16[8,128,256]{2,1,0:T(8,128)(2,1)} %bitcast.16), channel_id=1, source_target_pairs={{0,16},{8,24},{16,32},{24,40},{32,48},{40,56},{48,64},{56,72},{64,... | collective-permute-start | bytes 1572872 | tf_op jit(solution)/shard_map/ppermute | solution.py:183
  4.0 6.0 %collective-permute-start.1 = (bf16[8,128,256]{2,1,0:T(8,128)(2,1)}, bf16[8,128,256]{2,1,0:T(8,128)(2,1)S(1)}, u32[]{:S(2)}, u32[]{:S(2)}) collective-permute-start(bf16[8,128,256]{2,1,0:T(8,128)(2,1)} %bitcast.17), channel_id=1, source_target_pairs={{0,496},{8,504},{16,0},{24,8},{32,16},{40,24},{48,32},{56,40},{64,... | collective-permute-start | bytes 1572872 | tf_op jit(solution)/shard_map/ppermute | solution.py:184
  10.0 0.0 copy-start
  10.0 1.3 %tables.1 = (s32[2,128]{1,0:T(2,128)S(1)}, s32[1,128]{1,0:T(1,128)S(1)}, bf16[8,128,256]{2,1,0:T(8,128)(2,1)S(1)}) custom-call(s32[1]{0:T(128)} %bitcast.me_ref, s32[2,128]{1,0:T(2,128)} %bitcast.20, s32[4,128]{1,0:T(4,128)} %bitcast.19, bf16[8,128,256]{2,1,0:T(8,128)(2,1)} %bitcast.18), custom_call_target="tpu_custom_call" | custom-call | tf_op jit(solution)/shard_map/tables/pallas_call | solution.py:187
  11.3 3.5 %collective-permute-start.2 = (s32[1,128]{1,0:T(1,128)S(1)}, s32[1,128]{1,0:T(1,128)S(1)}, u32[]{:S(2)}, u32[]{:S(2)}) collective-permute-start(s32[1,128]{1,0:T(1,128)S(1)} %get-tuple-element.12.ids_in), channel_id=1, source_target_pairs={{0,496},{8,504},{16,0},{24,8},{32,16},{40,24},{48,32},{56,40},{64,... | collective-permute-start | bytes 1544 | tf_op jit(solution)/shard_map/ppermute | solution.py:204
  14.8 8.1 %collective-permute-start.3 = (s32[1,128]{1,0:T(1,128)S(1)}, s32[1,128]{1,0:T(1,128)S(1)}, u32[]{:S(2)}, u32[]{:S(2)}) collective-permute-start(s32[1,128]{1,0:T(1,128)S(1)} %get-tuple-element.12.ids_in), channel_id=1, source_target_pairs={{0,504},{8,16},{16,8},{24,32},{32,24},{40,48},{48,40},{56,64},{64,... | collective-permute-start | bytes 1544 | tf_op jit(solution)/shard_map/ppermute | solution.py:205
  22.9 1.9 %collective-permute-start.4 = (s32[1,128]{1,0:T(1,128)S(1)}, s32[1,128]{1,0:T(1,128)S(1)}, u32[]{:S(2)}, u32[]{:S(2)}) collective-permute-start(s32[1,128]{1,0:T(1,128)S(1)} %get-tuple-element.12.ids_in), channel_id=1, source_target_pairs={{0,8},{8,0},{16,24},{24,16},{32,40},{40,32},{48,56},{56,48},{64,72... | collective-permute-start | bytes 1544 | tf_op jit(solution)/shard_map/ppermute | solution.py:206
  24.8 0.0 collective-permute-done.2.ask_x
  24.8 0.0 collective-permute-done.3.ask_y
  24.8 1.1 %collective-permute-done.4.ask_n = s32[1,128]{1,0:T(1,128)S(1)} collective-permute-done((s32[1,128]{1,0:T(1,128)S(1)}, s32[1,128]{1,0:T(1,128)S(1)}, u32[]{:S(2)}, u32[]{:S(2)}) %collective-permute-start.4) | collective-permute-done | bytes 544 | tf_op jit(solution)/shard_map/ppermute | solution.py:206
  25.9 0.0 collective-permute-done.left
  25.9 0.0 collective-permute-done.1.right
  25.9 0.6 serve.1
  26.6 3.5 %collective-permute-start.7 = (bf16[6,128,256]{2,1,0:T(8,128)(2,1)S(1)}, bf16[6,128,256]{2,1,0:T(8,128)(2,1)S(1)}, u32[]{:S(2)}, u32[]{:S(2)}) collective-permute-start(bf16[6,128,256]{2,1,0:T(8,128)(2,1)S(1)} %get-tuple-element.16), channel_id=1, source_target_pairs={{0,8},{8,0},{16,24},{24,16},{32,40},{40,32},{48,56},{56,48},{64,72... | collective-permute-start | bytes 1179656 | tf_op jit(solution)/shard_map/ppermute | solution.py:231
  30.1 1.9 %collective-permute-start.5 = (bf16[2,128,256]{2,1,0:T(8,128)(2,1)S(1)}, bf16[2,128,256]{2,1,0:T(8,128)(2,1)S(1)}, u32[]{:S(2)}, u32[]{:S(2)}) collective-permute-start(bf16[2,128,256]{2,1,0:T(8,128)(2,1)S(1)} %get-tuple-element.14), channel_id=1, source_target_pairs={{0,16},{8,24},{16,32},{24,40},{32,48},{40,56},{48,64},{56,72},{64,... | collective-permute-start | bytes 393224 | tf_op jit(solution)/shard_map/ppermute | solution.py:229
  32.1 1.9 %collective-permute-start.6 = (bf16[2,128,256]{2,1,0:T(8,128)(2,1)S(1)}, bf16[2,128,256]{2,1,0:T(8,128)(2,1)S(1)}, u32[]{:S(2)}, u32[]{:S(2)}) collective-permute-start(bf16[2,128,256]{2,1,0:T(8,128)(2,1)S(1)} %get-tuple-element.15), channel_id=1, source_target_pairs={{0,504},{8,16},{16,8},{24,32},{32,24},{40,48},{48,40},{56,64},{64,... | collective-permute-start | bytes 393224 | tf_op jit(solution)/shard_map/ppermute | solution.py:230
  34.6 0.4 order.1.order_in
  35.0 5.4 %collective-permute-done.5.in_x = bf16[2,128,256]{2,1,0:T(8,128)(2,1)S(1)} collective-permute-done((bf16[2,128,256]{2,1,0:T(8,128)(2,1)S(1)}, bf16[2,128,256]{2,1,0:T(8,128)(2,1)S(1)}, u32[]{:S(2)}, u32[]{:S(2)}) %collective-permute-start.5) | collective-permute-done | bytes 131104 | tf_op jit(solution)/shard_map/ppermute | solution.py:229
  40.4 0.0 collective-permute-done.6.in_y
  40.4 0.0 collective-permute-done.7.in_n
  40.4 0.0 copy-done
  40.4 4.2 %project.1 = f32[256,256]{1,0:T(8,128)S(1)} custom-call(s32[8,256]{1,0:T(8,128)S(1)} %order.1.order_in, s32[1,128]{1,0:T(1,128)S(1)} %get-tuple-element.12.ids_in, bf16[128,128,128]{2,1,0:T(8,128)(2,1)S(1)} %copy-done, bf16[8,128,256]{2,1,0:T(8,128)(2,1)S(1)} %collective-permute-done.left, bf16[8,128,256]{2,1,0:T(8,128)(2,1)S(1)} %get-tuple-element.13.own, ...), custom_call_target="tpu_custom_call" | custom-call | tf_op jit(solution)/shard_map/project/pallas_call | solution.py:232
  44.6 19.0 %all_to_all.10 = f32[64,8,128]{2,1,0:T(8,128)S(1)} all-to-all(f32[64,8,128]{2,1,0:T(8,128)S(1)} %bitcast.14), channel_id=1, replica_groups=mesh['dom'=64,'grp'=8] {'dom'}, dimensions={0} | all-to-all | bytes 524288 | tf_op jit(solution)/shard_map/all_to_all | solution.py:248
  63.6 0.1 reduce_sum.9
  63.7 17.8 %all_to_all.11 = f32[64,8,128]{2,1,0:T(8,128)S(1)} all-to-all(f32[64,8,128]{2,1,0:T(8,128)S(1)} %broadcast_in_dim.3), channel_id=1, replica_groups=mesh['dom'=64,'grp'=8] {'dom'}, dimensions={0} | all-to-all | bytes 524288 | tf_op jit(solution)/shard_map/all_to_all | solution.py:251
  81.5 0.7 copy.8
  (1 shorter events, 0.0 us)
Async XLA Ops:
  0.0 25.9 %collective-permute-start = (bf16[8,128,256]{2,1,0:T(8,128)(2,1)}, bf16[8,128,256]{2,1,0:T(8,128)(2,1)S(1)}, u32[]{:S(2)}, u32[]{:S(2)}) collective-permute-start(bf16[8,128,256]{2,1,0:T(8,128)(2,1)} %bitcast.16), channel_id=1, source_target_pairs={{0,16},{8,24},{16,32},{24,40},{32,48},{40,56},{48,64},{56,72},{64,... | collective-permute-start | bytes 1572872 | tf_op jit(solution)/shard_map/ppermute | solution.py:183
  4.0 21.9 %collective-permute-start.1 = (bf16[8,128,256]{2,1,0:T(8,128)(2,1)}, bf16[8,128,256]{2,1,0:T(8,128)(2,1)S(1)}, u32[]{:S(2)}, u32[]{:S(2)}) collective-permute-start(bf16[8,128,256]{2,1,0:T(8,128)(2,1)} %bitcast.17), channel_id=1, source_target_pairs={{0,496},{8,504},{16,0},{24,8},{32,16},{40,24},{48,32},{56,40},{64,... | collective-permute-start | bytes 1572872 | tf_op jit(solution)/shard_map/ppermute | solution.py:184
  10.0 30.4 %copy-start = (bf16[128,128,128]{2,1,0:T(8,128)(2,1)S(1)}, bf16[128,128,128]{2,1,0:T(8,128)(2,1)}, u32[]{:S(2)}) copy-start(bf16[128,128,128]{2,1,0:T(8,128)(2,1)} %tiles.1) | copy-start | bytes 12582916
  11.3 13.5 %collective-permute-start.2 = (s32[1,128]{1,0:T(1,128)S(1)}, s32[1,128]{1,0:T(1,128)S(1)}, u32[]{:S(2)}, u32[]{:S(2)}) collective-permute-start(s32[1,128]{1,0:T(1,128)S(1)} %get-tuple-element.12.ids_in), channel_id=1, source_target_pairs={{0,496},{8,504},{16,0},{24,8},{32,16},{40,24},{48,32},{56,40},{64,... | collective-permute-start | bytes 1544 | tf_op jit(solution)/shard_map/ppermute | solution.py:204
  14.8 10.0 %collective-permute-start.3 = (s32[1,128]{1,0:T(1,128)S(1)}, s32[1,128]{1,0:T(1,128)S(1)}, u32[]{:S(2)}, u32[]{:S(2)}) collective-permute-start(s32[1,128]{1,0:T(1,128)S(1)} %get-tuple-element.12.ids_in), channel_id=1, source_target_pairs={{0,504},{8,16},{16,8},{24,32},{32,24},{40,48},{48,40},{56,64},{64,... | collective-permute-start | bytes 1544 | tf_op jit(solution)/shard_map/ppermute | solution.py:205
  22.9 3.1 %collective-permute-start.4 = (s32[1,128]{1,0:T(1,128)S(1)}, s32[1,128]{1,0:T(1,128)S(1)}, u32[]{:S(2)}, u32[]{:S(2)}) collective-permute-start(s32[1,128]{1,0:T(1,128)S(1)} %get-tuple-element.12.ids_in), channel_id=1, source_target_pairs={{0,8},{8,0},{16,24},{24,16},{32,40},{40,32},{48,56},{56,48},{64,72... | collective-permute-start | bytes 1544 | tf_op jit(solution)/shard_map/ppermute | solution.py:206
  26.6 13.8 %collective-permute-start.7 = (bf16[6,128,256]{2,1,0:T(8,128)(2,1)S(1)}, bf16[6,128,256]{2,1,0:T(8,128)(2,1)S(1)}, u32[]{:S(2)}, u32[]{:S(2)}) collective-permute-start(bf16[6,128,256]{2,1,0:T(8,128)(2,1)S(1)} %get-tuple-element.16), channel_id=1, source_target_pairs={{0,8},{8,0},{16,24},{24,16},{32,40},{40,32},{48,56},{56,48},{64,72... | collective-permute-start | bytes 1179656 | tf_op jit(solution)/shard_map/ppermute | solution.py:231
  30.1 10.3 %collective-permute-start.5 = (bf16[2,128,256]{2,1,0:T(8,128)(2,1)S(1)}, bf16[2,128,256]{2,1,0:T(8,128)(2,1)S(1)}, u32[]{:S(2)}, u32[]{:S(2)}) collective-permute-start(bf16[2,128,256]{2,1,0:T(8,128)(2,1)S(1)} %get-tuple-element.14), channel_id=1, source_target_pairs={{0,16},{8,24},{16,32},{24,40},{32,48},{40,56},{48,64},{56,72},{64,... | collective-permute-start | bytes 393224 | tf_op jit(solution)/shard_map/ppermute | solution.py:229
  32.1 8.3 %collective-permute-start.6 = (bf16[2,128,256]{2,1,0:T(8,128)(2,1)S(1)}, bf16[2,128,256]{2,1,0:T(8,128)(2,1)S(1)}, u32[]{:S(2)}, u32[]{:S(2)}) collective-permute-start(bf16[2,128,256]{2,1,0:T(8,128)(2,1)S(1)} %get-tuple-element.15), channel_id=1, source_target_pairs={{0,504},{8,16},{16,8},{24,32},{32,24},{40,48},{48,40},{56,64},{64,... | collective-permute-start | bytes 393224 | tf_op jit(solution)/shard_map/ppermute | solution.py:230

commit v2 on v1

--- a/solution.py
+++ b/solution.py
@@ -13,15 +13,13 @@
 UNROLL = 4
 
 
-def tables_kernel(me_ref, links_in, home_in, own, slots_ref, ids_ref, copy_ref, links_ref, home_ref, sems):
+def tables_kernel(me_ref, links_in, home_in, slots_ref, ids_ref, links_ref, home_ref, sems):
     loads = [
         pltpu.make_async_copy(links_in, links_ref, sems.at[0]),
         pltpu.make_async_copy(home_in, home_ref, sems.at[1]),
     ]
     for load in loads:
         load.start()
-    store = pltpu.make_async_copy(own, copy_ref, sems.at[2])
-    store.start()
     for load in loads:
         load.wait()
     me = me_ref[0]
@@ -58,10 +56,11 @@
     slots_ref[1:2, :] = col_slot
     ids = jnp.sum(jnp.where((wanted > 0.5) & (slot == lane), index % 8, 0), axis=0, keepdims=True)
     ids_ref[...] = ids
-    store.wait()
-
-
-def order_kernel(count_ref, slots_ref, order_ref):
+
+
+def order_kernel(count_ref, slots_ref, own, order_ref, copy_ref, sem):
+    store = pltpu.make_async_copy(own, copy_ref, sem)
+    store.start()
     tiles = slots_ref.shape[1]
     spots = order_ref.shape[1]
     rows = 2 * SLOTS
@@ -92,34 +91,47 @@
     n_groups = jnp.sum(groups[:, 0:1], axis=0, keepdims=True).astype(jnp.int32)
     found = jnp.where(kind == 1, found + SLOTS, found)
     order_ref[...] = jnp.where(kind == 3, n_groups, found)
-
-
-def serve_kernel(me_ref, ask_x, ask_y, ask_n, left, own, right, out_x, out_y, out_n, asked, sems):
+    store.wait()
+
+
+def serve_kernel(me_ref, ask_x, ask_y, ask_n, even, own, odd, out_x, out_y, out_n, asked, sems):
     core = me_ref[0] % 2
     fetch = [pltpu.make_async_copy(ask, asked.at[i], sems.at[i]) for i, ask in enumerate((ask_x, ask_y, ask_n))]
     for copy in fetch:
         copy.start()
     for copy in fetch:
         copy.wait()
-    for j in range(CAP):
-        out_x[j] = left[asked[0, 0, j]]
-
-    @pl.when(core == 0)
+
+    def fill(left, right):
+        for j in range(CAP):
+            out_x[j] = left[asked[0, 0, j]]
+            for n, source in enumerate((left, own, right)):
+                out_n[n * CAP + j] = source[asked[2, 0, (3 + 2 * n) * CAP + j]]
+
+        @pl.when(core == 0)
+        def _():
+            for j in range(CAP):
+                out_y[j] = right[asked[1, 0, CAP + j]]
+
+        @pl.when(core == 1)
+        def _():
+            for j in range(CAP):
+                out_y[j] = left[asked[1, 0, CAP + j]]
+
+    by_parity(me_ref[0], even, odd, fill)
+
+
+def by_parity(me, even, odd, use):
+    @pl.when((me // 2) % 2 == 0)
     def _():
-        for j in range(CAP):
-            out_y[j] = right[asked[1, 0, CAP + j]]
-
-    @pl.when(core == 1)
+        use(odd, even)
+
+    @pl.when((me // 2) % 2 == 1)
     def _():
-        for j in range(CAP):
-            out_y[j] = left[asked[1, 0, CAP + j]]
-
-    for n, source in enumerate((left, own, right)):
-        for j in range(CAP):
-            out_n[n * CAP + j] = source[asked[2, 0, (3 + 2 * n) * CAP + j]]
-
-
-def project_kernel(order_in, ids_in, tiles, left, own, right, in_x, in_y, in_n, out_ref,
+        use(even, odd)
+
+
+def project_kernel(me_ref, order_in, ids_in, tiles, even, own, odd, in_x, in_y, in_n, out_ref,
                    order, ids, blocks, sums, sems):
     block = tiles.shape[1]
     tabs = [pltpu.make_async_copy(order_in, order, sems.at[0]), pltpu.make_async_copy(ids_in, ids, sems.at[1])]
@@ -133,10 +145,14 @@
     sums[...] = jnp.zeros_like(sums)
     for copy in tabs:
         copy.wait()
-    for n, source in enumerate((left, own, right)):
-        for j in range(CAP):
-            spot = (2 + 2 * n) * CAP + j
-            blocks[spot] = source[ids[0, spot]]
+
+    def fill(left, right):
+        for n, source in enumerate((left, own, right)):
+            for j in range(CAP):
+                spot = (2 + 2 * n) * CAP + j
+                blocks[spot] = source[ids[0, spot]]
+
+    by_parity(me_ref[0], even, odd, fill)
 
     def step(s, carry):
         for k in range(UNROLL):
@@ -180,39 +196,39 @@
     def shift(steps):
         return [(i, (i + steps) % ndom) for i in range(ndom)]
 
-    left = lax.ppermute(own, "dom", shift(2))
-    right = lax.ppermute(own, "dom", shift(-2))
+    even = lax.ppermute(own, "dom", [(i, i ^ 2) for i in range(ndom)])
+    odd = lax.ppermute(own, "dom", [(i, (i + (2 if i & 2 else -2)) % ndom) for i in range(ndom)])
     stored = in_hbm(own)
     me = lax.axis_index("dom").astype(jnp.int32).reshape(1)
-    slots, ids, near = pl.pallas_call(
+    slots, ids = pl.pallas_call(
         tables_kernel,
         out_shape=(
             jax.ShapeDtypeStruct((2, n_tiles), jnp.int32),
             jax.ShapeDtypeStruct((1, n_tiles), jnp.int32),
-            jax.ShapeDtypeStruct(own.shape, bf16),
         ),
-        in_specs=[smem, anywhere, anywhere, anywhere],
-        out_specs=(vmem, vmem, vmem),
+        in_specs=[smem, anywhere, anywhere],
+        out_specs=(vmem, vmem),
         scratch_shapes=[
             pltpu.VMEM((2, n_tiles), jnp.int32),
             pltpu.VMEM((ndom * blk_dev // 128, 128), jnp.int32),
-            pltpu.SemaphoreType.DMA((3,)),
+            pltpu.SemaphoreType.DMA((2,)),
         ],
         compiler_params=pltpu.CompilerParams(vmem_limit_bytes=4 << 20),
         name="tables",
-    )(me, in_hbm(tile_blocks.T), in_hbm(block_home.reshape(-1, 128)), stored)
+    )(me, in_hbm(tile_blocks.T), in_hbm(block_home.reshape(-1, 128)))
     ask_x = lax.ppermute(ids, "dom", shift(-2))
     ask_y = lax.ppermute(ids, "dom", [(i, (i + (1 if i % 2 else -1)) % ndom) for i in range(ndom)])
     ask_n = lax.ppermute(ids, "dom", [(i, i ^ 1) for i in range(ndom)])
-    order = pl.pallas_call(
+    order, near = pl.pallas_call(
         order_kernel,
-        out_shape=jax.ShapeDtypeStruct((8, 2 * n_tiles), jnp.int32),
-        in_specs=[smem, vmem],
-        out_specs=vmem,
+        out_shape=(jax.ShapeDtypeStruct((8, 2 * n_tiles), jnp.int32), jax.ShapeDtypeStruct(own.shape, bf16)),
+        in_specs=[smem, vmem, anywhere],
+        out_specs=(vmem, vmem),
+        scratch_shapes=[pltpu.SemaphoreType.DMA],
         cost_estimate=pl.CostEstimate(flops=10**9, transcendentals=0, bytes_accessed=10**4),
         compiler_params=pltpu.CompilerParams(vmem_limit_bytes=4 << 20),
         name="order",
-    )(tile_count, slots)
+    )(tile_count, slots, stored)
 
     def blocks_of(count):
         return jax.ShapeDtypeStruct((count * CAP, block, rank), bf16)
@@ -225,14 +241,14 @@
         scratch_shapes=[pltpu.SMEM((3, 1, n_tiles), jnp.int32), pltpu.SemaphoreType.DMA((3,))],
         compiler_params=pltpu.CompilerParams(vmem_limit_bytes=8 << 20),
         name="serve",
-    )(me, ask_x, ask_y, ask_n, left, near, right)
+    )(me, ask_x, ask_y, ask_n, even, near, odd)
     in_x = lax.ppermute(out_x, "dom", shift(2))
     in_y = lax.ppermute(out_y, "dom", [(i, (i + (1 if i % 2 else -1)) % ndom) for i in range(ndom)])
     in_n = lax.ppermute(out_n, "dom", [(i, i ^ 1) for i in range(ndom)])
     partial_sum = pl.pallas_call(
         project_kernel,
         out_shape=jax.ShapeDtypeStruct((rank, rank), jnp.float32),
-        in_specs=[vmem] * 9,
+        in_specs=[smem] + [vmem] * 9,
         out_specs=vmem,
         scratch_shapes=[
             pltpu.SMEM((8, 2 * n_tiles), jnp.int32),
@@ -243,7 +259,7 @@
         ],
         compiler_params=pltpu.CompilerParams(vmem_limit_bytes=24 << 20),
         name="project",
-    )(order, ids, tangent_tiles, left, near, right, in_x, in_y, in_n)
+    )(me, order, ids, tangent_tiles, even, near, odd, in_x, in_y, in_n)
     cut = partial_sum.reshape(rank // 8, 8, rank // 128, 128).transpose(0, 2, 1, 3).reshape(ndom, 8, 128)
     parts = lax.all_to_all(cut, "dom", 0, 0, tiled=True)
     mine = jnp.sum(parts, axis=0)

time: 82.6 us -> 82.1 us (level)
  starting transfers between devices: 30.9 us -> 29.7 us
    ppermute x1, starting transfers between devices: 8.06 us -> 3.54 us  [on_device(): lax.ppermute(ids, 'dom', [(i, (i + (1 if i % 2 else -1)) % ndom) for i in...]
    ppermute x1, starting transfers between devices: 3.49 us -> 5.04 us  [on_device(): ask_x = lax.ppermute(ids, 'dom', shift(-2))]
    ppermute x1, waiting for transfers between devices: 5.37 us -> 6.51 us  [on_device(): in_x = lax.ppermute(out_x, 'dom', shift(2))]
    ppermute x1, waiting for transfers between devices: 1.11 us -> 0.01 us  [on_device(): ask_n = lax.ppermute(ids, 'dom', [(i, i ^ 1) for i in range(ndom)])]
    ppermute x1, starting transfers between devices: 1.92 us -> 3 us  [on_device(): ask_n = lax.ppermute(ids, 'dom', [(i, i ^ 1) for i in range(ndom)])]
  transfers between devices with their start and end apart: 8 -> 8, of which waited for: 2 -> 1; matrix products, arithmetic and copies ran while one was open for 0% -> 0% of each run, Pallas kernels for 2% -> 3%
where the time goes in v2:
time: 82.1 us; the launch traced here: 81.7 us
  blocking collectives  36.8 us (45%)
  starting transfers between devices  29.7 us (36%)
  Pallas kernels  6.97 us (8%)
  waiting for transfers between devices  6.52 us (8%)
    all_to_all x1, blocking collectives, on_device(): parts = lax.all_to_all(cut, 'dom', 0, 0, tiled=True)  19 us
    all_to_all x1, blocking collectives, on_device(): whole = lax.all_to_all(copies, 'dom', 0, 0, tiled=True)  17.8 us
    ppermute x1, starting transfers between devices, on_device(): lax.ppermute(own, 'dom', [(i, (i + (2 if i & 2 else -2)) % ndom) for i in...  8.1 us
    ppermute x1, waiting for transfers between devices, on_device(): in_x = lax.ppermute(out_x, 'dom', shift(2))  6.51 us
    ppermute x1, starting transfers between devices, on_device(): ask_x = lax.ppermute(ids, 'dom', shift(-2))  5.04 us
    ppermute x1, starting transfers between devices, on_device(): in_n = lax.ppermute(out_n, 'dom', [(i, i ^ 1) for i in range(ndom)])  4.3 us
    pallas_call x1, Pallas kernels, on_device(): pl.pallas_call(project_kernel, out_shape=jax.ShapeDtypeStruct((rank, rank...  4.06 us
    ppermute x1, starting transfers between devices, on_device(): lax.ppermute(ids, 'dom', [(i, (i + (1 if i % 2 else -1)) % ndom) for i in...  3.54 us
  transfers between devices with their start and end apart: 8, of which 1 were waited for; matrix products, arithmetic and copies ran while one was open for 0% of the time, Pallas kernels for 3%

profile of v2, /device:TPU:1, one launch (start us, length us, event | category | flops | bytes accessed | tf_op | source)
XLA Modules:
  0.0 81.7 jit_solution(11557619067170293594)
XLA Ops:
  0.0 8.1 %collective-permute-start.1 = (bf16[8,128,256]{2,1,0:T(8,128)(2,1)}, bf16[8,128,256]{2,1,0:T(8,128)(2,1)S(1)}, u32[]{:S(2)}, u32[]{:S(2)}) collective-permute-start(bf16[8,128,256]{2,1,0:T(8,128)(2,1)} %bitcast.18), channel_id=1, source_target_pairs={{0,496},{8,504},{16,32},{24,40},{32,16},{40,24},{48,64},{56,72},{6... | collective-permute-start | bytes 1572872 | tf_op jit(solution)/shard_map/ppermute | solution.py:200
  8.1 1.9 %collective-permute-start = (bf16[8,128,256]{2,1,0:T(8,128)(2,1)}, bf16[8,128,256]{2,1,0:T(8,128)(2,1)S(1)}, u32[]{:S(2)}, u32[]{:S(2)}) collective-permute-start(bf16[8,128,256]{2,1,0:T(8,128)(2,1)} %bitcast.19), channel_id=1, source_target_pairs={{0,16},{8,24},{16,0},{24,8},{32,48},{40,56},{48,32},{56,40},{64,80... | collective-permute-start | bytes 1572872 | tf_op jit(solution)/shard_map/ppermute | solution.py:199
  10.0 0.0 copy-start
  10.1 1.2 %tables.1 = (s32[2,128]{1,0:T(2,128)S(1)}, s32[1,128]{1,0:T(1,128)S(1)}) custom-call(s32[1]{0:T(128)} %bitcast.me_ref, s32[2,128]{1,0:T(2,128)} %bitcast.17, s32[4,128]{1,0:T(4,128)} %bitcast.16), custom_call_target="tpu_custom_call" | custom-call | tf_op jit(solution)/shard_map/tables/pallas_call | solution.py:203
  11.3 3.0 %collective-permute-start.4 = (s32[1,128]{1,0:T(1,128)S(1)}, s32[1,128]{1,0:T(1,128)S(1)}, u32[]{:S(2)}, u32[]{:S(2)}) collective-permute-start(s32[1,128]{1,0:T(1,128)S(1)} %get-tuple-element.14.ids_in), channel_id=1, source_target_pairs={{0,8},{8,0},{16,24},{24,16},{32,40},{40,32},{48,56},{56,48},{64,72... | collective-permute-start | bytes 1544 | tf_op jit(solution)/shard_map/ppermute | solution.py:221
  14.3 3.5 %collective-permute-start.3 = (s32[1,128]{1,0:T(1,128)S(1)}, s32[1,128]{1,0:T(1,128)S(1)}, u32[]{:S(2)}, u32[]{:S(2)}) collective-permute-start(s32[1,128]{1,0:T(1,128)S(1)} %get-tuple-element.14.ids_in), channel_id=1, source_target_pairs={{0,504},{8,16},{16,8},{24,32},{32,24},{40,48},{48,40},{56,64},{64,... | collective-permute-start | bytes 1544 | tf_op jit(solution)/shard_map/ppermute | solution.py:220
  17.8 5.0 %collective-permute-start.2 = (s32[1,128]{1,0:T(1,128)S(1)}, s32[1,128]{1,0:T(1,128)S(1)}, u32[]{:S(2)}, u32[]{:S(2)}) collective-permute-start(s32[1,128]{1,0:T(1,128)S(1)} %get-tuple-element.14.ids_in), channel_id=1, source_target_pairs={{0,496},{8,504},{16,0},{24,8},{32,16},{40,24},{48,32},{56,40},{64,... | collective-permute-start | bytes 1544 | tf_op jit(solution)/shard_map/ppermute | solution.py:219
  23.5 1.1 %order.1 = (s32[8,256]{1,0:T(8,128)S(1)}, bf16[8,128,256]{2,1,0:T(8,128)(2,1)S(1)}) custom-call(s32[1]{0:T(128)S(6)} %copy.7.count_ref, s32[2,128]{1,0:T(2,128)S(1)} %get-tuple-element.12.slots_ref, bf16[8,128,256]{2,1,0:T(8,128)(2,1)} %bitcast.20), custom_call_target="tpu_custom_call" | custom-call | flops 1000000000 | bytes 10000 | tf_op jit(solution)/shard_map/order/pallas_call | solution.py:222
  24.6 0.0 collective-permute-done.4.ask_n
  24.6 0.0 collective-permute-done.3.ask_y
  24.6 0.0 collective-permute-done.2.ask_x
  24.6 0.0 collective-permute-done.1.odd
  24.6 0.0 collective-permute-done.even
  24.6 0.7 serve.1
  25.3 4.3 %collective-permute-start.7 = (bf16[6,128,256]{2,1,0:T(8,128)(2,1)S(1)}, bf16[6,128,256]{2,1,0:T(8,128)(2,1)S(1)}, u32[]{:S(2)}, u32[]{:S(2)}) collective-permute-start(bf16[6,128,256]{2,1,0:T(8,128)(2,1)S(1)} %get-tuple-element.18), channel_id=1, source_target_pairs={{0,8},{8,0},{16,24},{24,16},{32,40},{40,32},{48,56},{56,48},{64,72... | collective-permute-start | bytes 1179656 | tf_op jit(solution)/shard_map/ppermute | solution.py:247
  29.6 1.9 %collective-permute-start.5 = (bf16[2,128,256]{2,1,0:T(8,128)(2,1)S(1)}, bf16[2,128,256]{2,1,0:T(8,128)(2,1)S(1)}, u32[]{:S(2)}, u32[]{:S(2)}) collective-permute-start(bf16[2,128,256]{2,1,0:T(8,128)(2,1)S(1)} %get-tuple-element.16), channel_id=1, source_target_pairs={{0,16},{8,24},{16,32},{24,40},{32,48},{40,56},{48,64},{56,72},{64,... | collective-permute-start | bytes 393224 | tf_op jit(solution)/shard_map/ppermute | solution.py:245
  31.5 1.9 %collective-permute-start.6 = (bf16[2,128,256]{2,1,0:T(8,128)(2,1)S(1)}, bf16[2,128,256]{2,1,0:T(8,128)(2,1)S(1)}, u32[]{:S(2)}, u32[]{:S(2)}) collective-permute-start(bf16[2,128,256]{2,1,0:T(8,128)(2,1)S(1)} %get-tuple-element.17), channel_id=1, source_target_pairs={{0,504},{8,16},{16,8},{24,32},{32,24},{40,48},{48,40},{56,64},{64,... | collective-permute-start | bytes 393224 | tf_op jit(solution)/shard_map/ppermute | solution.py:246
  33.5 6.5 %collective-permute-done.5.in_x = bf16[2,128,256]{2,1,0:T(8,128)(2,1)S(1)} collective-permute-done((bf16[2,128,256]{2,1,0:T(8,128)(2,1)S(1)}, bf16[2,128,256]{2,1,0:T(8,128)(2,1)S(1)}, u32[]{:S(2)}, u32[]{:S(2)}) %collective-permute-start.5) | collective-permute-done | bytes 131104 | tf_op jit(solution)/shard_map/ppermute | solution.py:245
  40.0 0.0 collective-permute-done.6.in_y
  40.0 0.0 collective-permute-done.7.in_n
  40.0 0.0 copy-done
  40.0 4.1 %project.1 = f32[256,256]{1,0:T(8,128)S(1)} custom-call(s32[1]{0:T(128)} %bitcast.me_ref, s32[8,256]{1,0:T(8,128)S(1)} %get-tuple-element.13.order_in, s32[1,128]{1,0:T(1,128)S(1)} %get-tuple-element.14.ids_in, bf16[128,128,128]{2,1,0:T(8,128)(2,1)S(1)} %copy-done, bf16[8,128,256]{2,1,0:T(8,128)(2,1)S(1)} %collective-permute-done.even, ...), custom_call_target="tpu_custom_call" | custom-call | tf_op jit(solution)/shard_map/project/pallas_call | solution.py:248
  44.0 19.0 %all_to_all.10 = f32[64,8,128]{2,1,0:T(8,128)S(1)} all-to-all(f32[64,8,128]{2,1,0:T(8,128)S(1)} %bitcast.14), channel_id=1, replica_groups=mesh['dom'=64,'grp'=8] {'dom'}, dimensions={0} | all-to-all | bytes 524288 | tf_op jit(solution)/shard_map/all_to_all | solution.py:264
  63.1 0.1 reduce_sum.9
  63.2 17.8 %all_to_all.11 = f32[64,8,128]{2,1,0:T(8,128)S(1)} all-to-all(f32[64,8,128]{2,1,0:T(8,128)S(1)} %broadcast_in_dim.3), channel_id=1, replica_groups=mesh['dom'=64,'grp'=8] {'dom'}, dimensions={0} | all-to-all | bytes 524288 | tf_op jit(solution)/shard_map/all_to_all | solution.py:267
  81.0 0.7 copy.8
  (1 shorter events, 0.0 us)
Async XLA Ops:
  0.0 24.6 %collective-permute-start.1 = (bf16[8,128,256]{2,1,0:T(8,128)(2,1)}, bf16[8,128,256]{2,1,0:T(8,128)(2,1)S(1)}, u32[]{:S(2)}, u32[]{:S(2)}) collective-permute-start(bf16[8,128,256]{2,1,0:T(8,128)(2,1)} %bitcast.18), channel_id=1, source_target_pairs={{0,496},{8,504},{16,32},{24,40},{32,16},{40,24},{48,64},{56,72},{6... | collective-permute-start | bytes 1572872 | tf_op jit(solution)/shard_map/ppermute | solution.py:200
  8.1 16.5 %collective-permute-start = (bf16[8,128,256]{2,1,0:T(8,128)(2,1)}, bf16[8,128,256]{2,1,0:T(8,128)(2,1)S(1)}, u32[]{:S(2)}, u32[]{:S(2)}) collective-permute-start(bf16[8,128,256]{2,1,0:T(8,128)(2,1)} %bitcast.19), channel_id=1, source_target_pairs={{0,16},{8,24},{16,0},{24,8},{32,48},{40,56},{48,32},{56,40},{64,80... | collective-permute-start | bytes 1572872 | tf_op jit(solution)/shard_map/ppermute | solution.py:199
  10.0 29.9 %copy-start = (bf16[128,128,128]{2,1,0:T(8,128)(2,1)S(1)}, bf16[128,128,128]{2,1,0:T(8,128)(2,1)}, u32[]{:S(2)}) copy-start(bf16[128,128,128]{2,1,0:T(8,128)(2,1)} %tiles.1) | copy-start | bytes 12582916
  11.3 13.3 %collective-permute-start.4 = (s32[1,128]{1,0:T(1,128)S(1)}, s32[1,128]{1,0:T(1,128)S(1)}, u32[]{:S(2)}, u32[]{:S(2)}) collective-permute-start(s32[1,128]{1,0:T(1,128)S(1)} %get-tuple-element.14.ids_in), channel_id=1, source_target_pairs={{0,8},{8,0},{16,24},{24,16},{32,40},{40,32},{48,56},{56,48},{64,72... | collective-permute-start | bytes 1544 | tf_op jit(solution)/shard_map/ppermute | solution.py:221
  14.3 10.3 %collective-permute-start.3 = (s32[1,128]{1,0:T(1,128)S(1)}, s32[1,128]{1,0:T(1,128)S(1)}, u32[]{:S(2)}, u32[]{:S(2)}) collective-permute-start(s32[1,128]{1,0:T(1,128)S(1)} %get-tuple-element.14.ids_in), channel_id=1, source_target_pairs={{0,504},{8,16},{16,8},{24,32},{32,24},{40,48},{48,40},{56,64},{64,... | collective-permute-start | bytes 1544 | tf_op jit(solution)/shard_map/ppermute | solution.py:220
  17.8 6.8 %collective-permute-start.2 = (s32[1,128]{1,0:T(1,128)S(1)}, s32[1,128]{1,0:T(1,128)S(1)}, u32[]{:S(2)}, u32[]{:S(2)}) collective-permute-start(s32[1,128]{1,0:T(1,128)S(1)} %get-tuple-element.14.ids_in), channel_id=1, source_target_pairs={{0,496},{8,504},{16,0},{24,8},{32,16},{40,24},{48,32},{56,40},{64,... | collective-permute-start | bytes 1544 | tf_op jit(solution)/shard_map/ppermute | solution.py:219
  25.3 14.7 %collective-permute-start.7 = (bf16[6,128,256]{2,1,0:T(8,128)(2,1)S(1)}, bf16[6,128,256]{2,1,0:T(8,128)(2,1)S(1)}, u32[]{:S(2)}, u32[]{:S(2)}) collective-permute-start(bf16[6,128,256]{2,1,0:T(8,128)(2,1)S(1)} %get-tuple-element.18), channel_id=1, source_target_pairs={{0,8},{8,0},{16,24},{24,16},{32,40},{40,32},{48,56},{56,48},{64,72... | collective-permute-start | bytes 1179656 | tf_op jit(solution)/shard_map/ppermute | solution.py:247
  29.6 10.4 %collective-permute-start.5 = (bf16[2,128,256]{2,1,0:T(8,128)(2,1)S(1)}, bf16[2,128,256]{2,1,0:T(8,128)(2,1)S(1)}, u32[]{:S(2)}, u32[]{:S(2)}) collective-permute-start(bf16[2,128,256]{2,1,0:T(8,128)(2,1)S(1)} %get-tuple-element.16), channel_id=1, source_target_pairs={{0,16},{8,24},{16,32},{24,40},{32,48},{40,56},{48,64},{56,72},{64,... | collective-permute-start | bytes 393224 | tf_op jit(solution)/shard_map/ppermute | solution.py:245
  31.5 8.4 %collective-permute-start.6 = (bf16[2,128,256]{2,1,0:T(8,128)(2,1)S(1)}, bf16[2,128,256]{2,1,0:T(8,128)(2,1)S(1)}, u32[]{:S(2)}, u32[]{:S(2)}) collective-permute-start(bf16[2,128,256]{2,1,0:T(8,128)(2,1)S(1)} %get-tuple-element.17), channel_id=1, source_target_pairs={{0,504},{8,16},{16,8},{24,32},{32,24},{40,48},{48,40},{56,64},{64,... | collective-permute-start | bytes 393224 | tf_op jit(solution)/shard_map/ppermute | solution.py:246

commit v3 on v2

--- a/solution.py
+++ b/solution.py
@@ -9,8 +9,8 @@
 CAP = 2
 NEAR = 8
 SLOTS = NEAR * CAP
-GROUP = 4
-UNROLL = 4
+GROUP = 2
+UNROLL = 24
 
 
 def tables_kernel(me_ref, links_in, home_in, slots_ref, ids_ref, links_ref, home_ref, sems):
@@ -263,9 +263,10 @@
     cut = partial_sum.reshape(rank // 8, 8, rank // 128, 128).transpose(0, 2, 1, 3).reshape(ndom, 8, 128)
     parts = lax.all_to_all(cut, "dom", 0, 0, tiled=True)
     mine = jnp.sum(parts, axis=0)
-    copies = jnp.broadcast_to(mine, (ndom, 8, 128))
+    copies = jnp.broadcast_to(mine.astype(bf16), (ndom, 8, 128))
     whole = lax.all_to_all(copies, "dom", 0, 0, tiled=True)
-    return whole.reshape(rank // 8, rank // 128, 8, 128).transpose(0, 2, 1, 3).reshape(rank, rank)
+    whole = whole.reshape(rank // 8, rank // 128, 8, 128).transpose(0, 2, 1, 3).reshape(rank, rank)
+    return whole.astype(jnp.float32)
 
 
 def solution(mesh):

time: 82.1 us -> 80.5 us (0.981)
  blocking collectives: 36.8 us -> 35.3 us
    all_to_all x1, blocking collectives: 17.8 us -> 16.2 us  [on_device(): whole = lax.all_to_all(copies, 'dom', 0, 0, tiled=True)]
where the time goes in v3:
time: 80.5 us; the launch traced here: 80.1 us
  blocking collectives  35.3 us (44%)
  starting transfers between devices  29.7 us (37%)
  Pallas kernels  6.85 us (9%)
  waiting for transfers between devices  6.52 us (8%)
  between operations  0.81 us (1%)
    all_to_all x1, blocking collectives, on_device(): parts = lax.all_to_all(cut, 'dom', 0, 0, tiled=True)  19.2 us
    all_to_all x1, blocking collectives, on_device(): whole = lax.all_to_all(copies, 'dom', 0, 0, tiled=True)  16.2 us
    ppermute x1, starting transfers between devices, on_device(): lax.ppermute(own, 'dom', [(i, (i + (2 if i & 2 else -2)) % ndom) for i in...  8.1 us
    ppermute x1, waiting for transfers between devices, on_device(): in_x = lax.ppermute(out_x, 'dom', shift(2))  6.51 us
    ppermute x1, starting transfers between devices, on_device(): ask_x = lax.ppermute(ids, 'dom', shift(-2))  5.04 us
    ppermute x1, starting transfers between devices, on_device(): in_n = lax.ppermute(out_n, 'dom', [(i, i ^ 1) for i in range(ndom)])  4.3 us
    pallas_call x1, Pallas kernels, on_device(): pl.pallas_call(project_kernel, out_shape=jax.ShapeDtypeStruct((rank, rank...  3.94 us
    ppermute x1, starting transfers between devices, on_device(): lax.ppermute(ids, 'dom', [(i, (i + (1 if i % 2 else -1)) % ndom) for i in...  3.54 us
  transfers between devices with their start and end apart: 8, of which 1 were waited for; matrix products, arithmetic and copies ran while one was open for 0% of the time, Pallas kernels for 3%

profile of v3, /device:TPU:1, one launch (start us, length us, event | category | flops | bytes accessed | tf_op | source)
XLA Modules:
  0.0 80.1 jit_solution(11583495385191428615)
XLA Ops:
  0.0 8.1 %collective-permute-start.1 = (bf16[8,128,256]{2,1,0:T(8,128)(2,1)}, bf16[8,128,256]{2,1,0:T(8,128)(2,1)S(1)}, u32[]{:S(2)}, u32[]{:S(2)}) collective-permute-start(bf16[8,128,256]{2,1,0:T(8,128)(2,1)} %bitcast.19), channel_id=1, source_target_pairs={{0,496},{8,504},{16,32},{24,40},{32,16},{40,24},{48,64},{56,72},{6... | collective-permute-start | bytes 1572872 | tf_op jit(solution)/shard_map/ppermute | solution.py:200
  8.1 1.9 %collective-permute-start = (bf16[8,128,256]{2,1,0:T(8,128)(2,1)}, bf16[8,128,256]{2,1,0:T(8,128)(2,1)S(1)}, u32[]{:S(2)}, u32[]{:S(2)}) collective-permute-start(bf16[8,128,256]{2,1,0:T(8,128)(2,1)} %bitcast.20), channel_id=1, source_target_pairs={{0,16},{8,24},{16,0},{24,8},{32,48},{40,56},{48,32},{56,40},{64,80... | collective-permute-start | bytes 1572872 | tf_op jit(solution)/shard_map/ppermute | solution.py:199
  10.0 0.0 copy-start
  10.1 1.2 %tables.1 = (s32[2,128]{1,0:T(2,128)S(1)}, s32[1,128]{1,0:T(1,128)S(1)}) custom-call(s32[1]{0:T(128)} %bitcast.me_ref, s32[2,128]{1,0:T(2,128)} %bitcast.18, s32[4,128]{1,0:T(4,128)} %bitcast.17), custom_call_target="tpu_custom_call" | custom-call | tf_op jit(solution)/shard_map/tables/pallas_call | solution.py:203
  11.3 3.0 %collective-permute-start.4 = (s32[1,128]{1,0:T(1,128)S(1)}, s32[1,128]{1,0:T(1,128)S(1)}, u32[]{:S(2)}, u32[]{:S(2)}) collective-permute-start(s32[1,128]{1,0:T(1,128)S(1)} %get-tuple-element.14.ids_in), channel_id=1, source_target_pairs={{0,8},{8,0},{16,24},{24,16},{32,40},{40,32},{48,56},{56,48},{64,72... | collective-permute-start | bytes 1544 | tf_op jit(solution)/shard_map/ppermute | solution.py:221
  14.3 3.5 %collective-permute-start.3 = (s32[1,128]{1,0:T(1,128)S(1)}, s32[1,128]{1,0:T(1,128)S(1)}, u32[]{:S(2)}, u32[]{:S(2)}) collective-permute-start(s32[1,128]{1,0:T(1,128)S(1)} %get-tuple-element.14.ids_in), channel_id=1, source_target_pairs={{0,504},{8,16},{16,8},{24,32},{32,24},{40,48},{48,40},{56,64},{64,... | collective-permute-start | bytes 1544 | tf_op jit(solution)/shard_map/ppermute | solution.py:220
  17.8 5.0 %collective-permute-start.2 = (s32[1,128]{1,0:T(1,128)S(1)}, s32[1,128]{1,0:T(1,128)S(1)}, u32[]{:S(2)}, u32[]{:S(2)}) collective-permute-start(s32[1,128]{1,0:T(1,128)S(1)} %get-tuple-element.14.ids_in), channel_id=1, source_target_pairs={{0,496},{8,504},{16,0},{24,8},{32,16},{40,24},{48,32},{56,40},{64,... | collective-permute-start | bytes 1544 | tf_op jit(solution)/shard_map/ppermute | solution.py:219
  23.5 1.1 %order.1 = (s32[8,256]{1,0:T(8,128)S(1)}, bf16[8,128,256]{2,1,0:T(8,128)(2,1)S(1)}) custom-call(s32[1]{0:T(128)S(6)} %copy.6.count_ref, s32[2,128]{1,0:T(2,128)S(1)} %get-tuple-element.12.slots_ref, bf16[8,128,256]{2,1,0:T(8,128)(2,1)} %bitcast.21), custom_call_target="tpu_custom_call" | custom-call | flops 1000000000 | bytes 10000 | tf_op jit(solution)/shard_map/order/pallas_call | solution.py:222
  24.6 0.0 collective-permute-done.4.ask_n
  24.6 0.0 collective-permute-done.3.ask_y
  24.6 0.0 collective-permute-done.2.ask_x
  24.6 0.0 collective-permute-done.1.odd
  24.6 0.0 collective-permute-done.even
  24.6 0.7 serve.1
  25.3 4.3 %collective-permute-start.7 = (bf16[6,128,256]{2,1,0:T(8,128)(2,1)S(1)}, bf16[6,128,256]{2,1,0:T(8,128)(2,1)S(1)}, u32[]{:S(2)}, u32[]{:S(2)}) collective-permute-start(bf16[6,128,256]{2,1,0:T(8,128)(2,1)S(1)} %get-tuple-element.18), channel_id=1, source_target_pairs={{0,8},{8,0},{16,24},{24,16},{32,40},{40,32},{48,56},{56,48},{64,72... | collective-permute-start | bytes 1179656 | tf_op jit(solution)/shard_map/ppermute | solution.py:247
  29.6 1.9 %collective-permute-start.5 = (bf16[2,128,256]{2,1,0:T(8,128)(2,1)S(1)}, bf16[2,128,256]{2,1,0:T(8,128)(2,1)S(1)}, u32[]{:S(2)}, u32[]{:S(2)}) collective-permute-start(bf16[2,128,256]{2,1,0:T(8,128)(2,1)S(1)} %get-tuple-element.16), channel_id=1, source_target_pairs={{0,16},{8,24},{16,32},{24,40},{32,48},{40,56},{48,64},{56,72},{64,... | collective-permute-start | bytes 393224 | tf_op jit(solution)/shard_map/ppermute | solution.py:245
  31.5 1.9 %collective-permute-start.6 = (bf16[2,128,256]{2,1,0:T(8,128)(2,1)S(1)}, bf16[2,128,256]{2,1,0:T(8,128)(2,1)S(1)}, u32[]{:S(2)}, u32[]{:S(2)}) collective-permute-start(bf16[2,128,256]{2,1,0:T(8,128)(2,1)S(1)} %get-tuple-element.17), channel_id=1, source_target_pairs={{0,504},{8,16},{16,8},{24,32},{32,24},{40,48},{48,40},{56,64},{64,... | collective-permute-start | bytes 393224 | tf_op jit(solution)/shard_map/ppermute | solution.py:246
  33.5 6.5 %collective-permute-done.5.in_x = bf16[2,128,256]{2,1,0:T(8,128)(2,1)S(1)} collective-permute-done((bf16[2,128,256]{2,1,0:T(8,128)(2,1)S(1)}, bf16[2,128,256]{2,1,0:T(8,128)(2,1)S(1)}, u32[]{:S(2)}, u32[]{:S(2)}) %collective-permute-start.5) | collective-permute-done | bytes 131104 | tf_op jit(solution)/shard_map/ppermute | solution.py:245
  40.0 0.0 collective-permute-done.6.in_y
  40.0 0.0 collective-permute-done.7.in_n
  40.0 0.0 copy-done
  40.0 3.9 %project.1 = f32[256,256]{1,0:T(8,128)S(1)} custom-call(s32[1]{0:T(128)} %bitcast.me_ref, s32[8,256]{1,0:T(8,128)S(1)} %get-tuple-element.13.order_in, s32[1,128]{1,0:T(1,128)S(1)} %get-tuple-element.14.ids_in, bf16[128,128,128]{2,1,0:T(8,128)(2,1)S(1)} %copy-done, bf16[8,128,256]{2,1,0:T(8,128)(2,1)S(1)} %collective-permute-done.even, ...), custom_call_target="tpu_custom_call" | custom-call | tf_op jit(solution)/shard_map/project/pallas_call | solution.py:248
  43.9 19.2 %all_to_all.10 = f32[64,8,128]{2,1,0:T(8,128)S(1)} all-to-all(f32[64,8,128]{2,1,0:T(8,128)S(1)} %bitcast.15), channel_id=1, replica_groups=mesh['dom'=64,'grp'=8] {'dom'}, dimensions={0} | all-to-all | bytes 524288 | tf_op jit(solution)/shard_map/all_to_all | solution.py:264
  63.1 0.1 reduce_sum.9
  63.2 16.2 %all_to_all.11 = bf16[64,8,128]{2,1,0:T(8,128)(2,1)S(1)} all-to-all(bf16[64,8,128]{2,1,0:T(8,128)(2,1)S(1)} %broadcast_in_dim.3), channel_id=1, replica_groups=mesh['dom'=64,'grp'=8] {'dom'}, dimensions={0} | all-to-all | bytes 262144 | tf_op jit(solution)/shard_map/all_to_all | solution.py:267
  79.4 0.7 convert_bitcast_fusion
  (1 shorter events, 0.0 us)
Async XLA Ops:
  0.0 24.6 %collective-permute-start.1 = (bf16[8,128,256]{2,1,0:T(8,128)(2,1)}, bf16[8,128,256]{2,1,0:T(8,128)(2,1)S(1)}, u32[]{:S(2)}, u32[]{:S(2)}) collective-permute-start(bf16[8,128,256]{2,1,0:T(8,128)(2,1)} %bitcast.19), channel_id=1, source_target_pairs={{0,496},{8,504},{16,32},{24,40},{32,16},{40,24},{48,64},{56,72},{6... | collective-permute-start | bytes 1572872 | tf_op jit(solution)/shard_map/ppermute | solution.py:200
  8.1 16.5 %collective-permute-start = (bf16[8,128,256]{2,1,0:T(8,128)(2,1)}, bf16[8,128,256]{2,1,0:T(8,128)(2,1)S(1)}, u32[]{:S(2)}, u32[]{:S(2)}) collective-permute-start(bf16[8,128,256]{2,1,0:T(8,128)(2,1)} %bitcast.20), channel_id=1, source_target_pairs={{0,16},{8,24},{16,0},{24,8},{32,48},{40,56},{48,32},{56,40},{64,80... | collective-permute-start | bytes 1572872 | tf_op jit(solution)/shard_map/ppermute | solution.py:199
  10.0 29.9 %copy-start = (bf16[128,128,128]{2,1,0:T(8,128)(2,1)S(1)}, bf16[128,128,128]{2,1,0:T(8,128)(2,1)}, u32[]{:S(2)}) copy-start(bf16[128,128,128]{2,1,0:T(8,128)(2,1)} %tiles.1) | copy-start | bytes 12582916
  11.3 13.3 %collective-permute-start.4 = (s32[1,128]{1,0:T(1,128)S(1)}, s32[1,128]{1,0:T(1,128)S(1)}, u32[]{:S(2)}, u32[]{:S(2)}) collective-permute-start(s32[1,128]{1,0:T(1,128)S(1)} %get-tuple-element.14.ids_in), channel_id=1, source_target_pairs={{0,8},{8,0},{16,24},{24,16},{32,40},{40,32},{48,56},{56,48},{64,72... | collective-permute-start | bytes 1544 | tf_op jit(solution)/shard_map/ppermute | solution.py:221
  14.3 10.3 %collective-permute-start.3 = (s32[1,128]{1,0:T(1,128)S(1)}, s32[1,128]{1,0:T(1,128)S(1)}, u32[]{:S(2)}, u32[]{:S(2)}) collective-permute-start(s32[1,128]{1,0:T(1,128)S(1)} %get-tuple-element.14.ids_in), channel_id=1, source_target_pairs={{0,504},{8,16},{16,8},{24,32},{32,24},{40,48},{48,40},{56,64},{64,... | collective-permute-start | bytes 1544 | tf_op jit(solution)/shard_map/ppermute | solution.py:220
  17.8 6.8 %collective-permute-start.2 = (s32[1,128]{1,0:T(1,128)S(1)}, s32[1,128]{1,0:T(1,128)S(1)}, u32[]{:S(2)}, u32[]{:S(2)}) collective-permute-start(s32[1,128]{1,0:T(1,128)S(1)} %get-tuple-element.14.ids_in), channel_id=1, source_target_pairs={{0,496},{8,504},{16,0},{24,8},{32,16},{40,24},{48,32},{56,40},{64,... | collective-permute-start | bytes 1544 | tf_op jit(solution)/shard_map/ppermute | solution.py:219
  25.3 14.7 %collective-permute-start.7 = (bf16[6,128,256]{2,1,0:T(8,128)(2,1)S(1)}, bf16[6,128,256]{2,1,0:T(8,128)(2,1)S(1)}, u32[]{:S(2)}, u32[]{:S(2)}) collective-permute-start(bf16[6,128,256]{2,1,0:T(8,128)(2,1)S(1)} %get-tuple-element.18), channel_id=1, source_target_pairs={{0,8},{8,0},{16,24},{24,16},{32,40},{40,32},{48,56},{56,48},{64,72... | collective-permute-start | bytes 1179656 | tf_op jit(solution)/shard_map/ppermute | solution.py:247
  29.6 10.4 %collective-permute-start.5 = (bf16[2,128,256]{2,1,0:T(8,128)(2,1)S(1)}, bf16[2,128,256]{2,1,0:T(8,128)(2,1)S(1)}, u32[]{:S(2)}, u32[]{:S(2)}) collective-permute-start(bf16[2,128,256]{2,1,0:T(8,128)(2,1)S(1)} %get-tuple-element.16), channel_id=1, source_target_pairs={{0,16},{8,24},{16,32},{24,40},{32,48},{40,56},{48,64},{56,72},{64,... | collective-permute-start | bytes 393224 | tf_op jit(solution)/shard_map/ppermute | solution.py:245
  31.5 8.4 %collective-permute-start.6 = (bf16[2,128,256]{2,1,0:T(8,128)(2,1)S(1)}, bf16[2,128,256]{2,1,0:T(8,128)(2,1)S(1)}, u32[]{:S(2)}, u32[]{:S(2)}) collective-permute-start(bf16[2,128,256]{2,1,0:T(8,128)(2,1)S(1)} %get-tuple-element.17), channel_id=1, source_target_pairs={{0,504},{8,16},{16,8},{24,32},{32,24},{40,48},{48,40},{56,64},{64,... | collective-permute-start | bytes 393224 | tf_op jit(solution)/shard_map/ppermute | solution.py:246
